TPU v7x, 512 devices: a whole 4x4x16 slice. The times are simulated.
512 devices in a mesh: dp: 16 (over y, x), space: 32 (over z, core).
Axes of the slice: x: 4, y: 4, z: 16, core: 2. Of those that a mesh axis runs over, the one named last changes fastest.
Arguments:
- voxel_feats: bfloat16 [16, 4096, 256], P('dp', 'space'), may hold values from -6 to 6
- neighbours: int32 [16, 4096, 6], P('dp', 'space'), may hold values from 0 to 384
- wanted_rows: int32 [16, 32, 32, 8], P('dp', 'space'), may hold values from 0 to 127
- live_counts: int32 [16, 32], P('dp'), may hold values from 1 to 128, 3072 in all within a row
- block_choice: int32 [16, 64, 4], P('dp', 'space'), may hold values from 0 to 63, all different within a row
- conv_weight: bfloat16 [7, 256, 512], P(None, 'space'), may hold values from -0.125 to 0.125
- norm_gain: float32 [512], replicated, may hold values from 0.1 to 1.9
- input_weight: bfloat16 [512, 2304], P('space'), may hold values from -5 to 5
- output_weight: bfloat16 [768, 512], P('space'), may hold values from -0.21875 to 0.21875
- cotangent: bfloat16 [16, 4096, 512], P('dp', 'space'), may hold values from -6 to 6
Outputs:
- layer_output: bfloat16 [16, 4096, 512], P('dp', 'space')
- output_grad: float32 [768, 512], P('space')
Inputs may be any that keep to these rules, and one draw needn't show every extreme that they name: `neighbours`: an entry below 128 names a row of the device's own shard, entry 128 + p * 8 + c names the row taken from peer p in slot c, and the largest value names an absent neighbour. `wanted_rows`: places within the peer's shard. `block_choice`: each row names distinct blocks.
All inputs are finite; a program needn't handle non-finite values.
Results may differ from a plain program's by a relative error of at most 0.025.
Values may be sent and summed in bfloat16 or wider, within the bound.
A program may use at most 64 MiB of HBM per device.

v0:
```python
import jax
import jax.numpy as jnp
from jax import lax
from jax.sharding import Mesh
from jax.sharding import PartitionSpec as P

HEADS = 12
HEAD_DIM = 64
BLK = 64
SEL = 4
SPACE = ("space_0", "space_1")


def in_order(parts, dim):
    parts = jnp.moveaxis(parts, 0, dim)
    shape = parts.shape
    return parts.reshape(*shape[:dim], shape[dim] * shape[dim + 1], *shape[dim + 2 :])


def gather_in_order(x, axes, turns):
    parts = x[None]
    for k in turns:
        parts = lax.all_gather(parts, axes[k], axis=0, tiled=True)
    held = [lax.axis_size(axes[k]) for k in reversed(turns)]
    parts = parts.reshape(*held, *x.shape)
    turned = sorted(range(len(turns)), key=lambda place: turns[len(turns) - 1 - place])
    return parts.transpose(*turned, *range(len(turns), parts.ndim)).reshape(-1, *x.shape)


def gather_axes(x, axes, turns, dim):
    return in_order(gather_in_order(x, axes, turns), dim)


def in_one_piece(arrays, axis, dim, along):
    ends, at = ([], 0)
    for a in arrays[:-1]:
        at += a.shape[along]
        ends.append(at)
    both = jnp.concatenate(arrays, axis=along)
    return tuple(jnp.split(lax.all_gather(both, axis, axis=dim, tiled=True), ends, axis=along))


def in_blocks(x, dim, peers):
    shape = x.shape
    parts = x.reshape(*shape[:dim], peers, shape[dim] // peers, *shape[dim + 1 :])
    return jnp.moveaxis(parts, dim, 0)


def sent_and_summed(x, axis, dim):
    parts = in_blocks(x, dim, lax.axis_size(axis))
    arrived = lax.all_to_all(parts, axis, split_axis=0, concat_axis=0, tiled=True)
    return arrived.astype(jnp.float32).sum(axis=0)


def sent_to_all(x, axis):
    copies = jnp.broadcast_to(x, (lax.axis_size(axis), *x.shape))
    return lax.all_to_all(copies, axis, split_axis=0, concat_axis=0, tiled=True)


def over_copies(x, axis):
    everything = sent_to_all(x, axis)
    return jnp.sum(everything.astype(jnp.float32), axis=0)


def attend(query, keys, values, key_live, short_keys, short_values):
    scale = HEAD_DIM ** (-0.5)
    near = jnp.einsum("bqhd,bkhd->bhqk", query, keys, preferred_element_type=jnp.float32) * scale
    near = jnp.where(key_live[:, None, None, :], near, -1e30)
    far = (
        jnp.einsum("bqhd,bshd->bhqs", query, short_keys, preferred_element_type=jnp.float32) * scale
    )
    scores = jnp.concatenate([near, far], axis=-1)
    highest = jnp.max(scores, axis=-1, keepdims=True)
    weights = jnp.exp(scores - highest)
    weights = (weights / jnp.sum(weights, axis=-1, keepdims=True)).astype(jnp.bfloat16)
    mixed = jnp.einsum(
        "bhqk,bkhd->bqhd", weights[..., :BLK], values, preferred_element_type=jnp.float32
    )
    return mixed + jnp.einsum(
        "bhqs,bshd->bqhd", weights[..., BLK:], short_values, preferred_element_type=jnp.float32
    )


def shards(
    voxel_feats,
    neighbours,
    wanted_rows,
    live_counts,
    block_choice,
    conv_weight,
    norm_gain,
    input_weight,
    output_weight,
    cotangent,
):
    space_count = lax.axis_size(SPACE)
    position = lax.axis_index(SPACE)
    own_rows = voxel_feats[0]
    shard_rows = own_rows.shape[0]
    index_map = neighbours[0]
    zero_row = jnp.zeros((1, own_rows.shape[1]), jnp.bfloat16)
    requested = lax.all_to_all(wanted_rows[0, 0], SPACE, split_axis=0, concat_axis=0, tiled=True)
    answers = own_rows[requested]
    arrived = lax.all_to_all(answers, SPACE, split_axis=0, concat_axis=0, tiled=True)
    padded = jnp.concatenate([own_rows, arrived.reshape(-1, own_rows.shape[1]), zero_row], axis=0)
    gathered_taps = padded[index_map]
    table = jnp.concatenate([own_rows[:, None, :], gathered_taps], axis=1)
    columns = table
    hidden = jnp.einsum(
        "tkr,kro->to",
        columns,
        gather_axes(conv_weight, SPACE, (0, 1), 1),
        preferred_element_type=jnp.float32,
    )
    live_count = lax.dynamic_index_in_dim(live_counts[0], position, keepdims=False)
    live = jnp.arange(shard_rows, dtype=jnp.int32) < live_count
    live_f = live.astype(jnp.float32)
    hidden = hidden * live_f[:, None]
    power = jnp.mean(hidden * hidden, axis=-1, keepdims=True)
    normed = (hidden * lax.rsqrt(power + 1e-06) * norm_gain).astype(jnp.bfloat16)
    columns = normed
    projected = jnp.dot(
        columns, gather_axes(input_weight, SPACE, (0, 1), 0), preferred_element_type=jnp.float32
    ).astype(jnp.bfloat16)
    att_width = input_weight.shape[1] // 3
    local_blocks = shard_rows // BLK
    query = projected[:, :att_width].reshape(local_blocks, BLK, HEADS, HEAD_DIM)
    keys = projected[:, att_width : 2 * att_width]
    values = projected[:, 2 * att_width :]
    block_live = live_f.reshape(local_blocks, BLK)
    divisor = jnp.maximum(jnp.sum(block_live, axis=1), 1.0)[:, None]
    short_keys = (
        jnp.sum(
            keys.astype(jnp.float32).reshape(local_blocks, BLK, att_width) * block_live[:, :, None],
            axis=1,
        )
        / divisor
    ).astype(jnp.bfloat16)
    short_values = (
        jnp.sum(
            values.astype(jnp.float32).reshape(local_blocks, BLK, att_width)
            * block_live[:, :, None],
            axis=1,
        )
        / divisor
    ).astype(jnp.bfloat16)
    every_keys, every_values = in_one_piece((short_keys, short_values), SPACE, 0, 1)
    chosen = block_choice[0]
    picked_keys = every_keys[chosen].reshape(local_blocks, SEL, HEADS, HEAD_DIM)
    picked_values = every_values[chosen].reshape(local_blocks, SEL, HEADS, HEAD_DIM)
    mixed = attend(
        query,
        keys.reshape(local_blocks, BLK, HEADS, HEAD_DIM),
        values.reshape(local_blocks, BLK, HEADS, HEAD_DIM),
        live.reshape(local_blocks, BLK),
        picked_keys,
        picked_values,
    )
    attended = (mixed.reshape(shard_rows, att_width) * live_f[:, None]).astype(jnp.bfloat16)
    columns = attended
    projected_out = jnp.dot(
        columns, gather_axes(output_weight, SPACE, (0, 1), 0), preferred_element_type=jnp.float32
    )
    layer = (hidden + projected_out).astype(jnp.bfloat16)[None]
    upstream = cotangent[0]
    factor = (lax.axis_size("dp") * space_count * shard_rows) ** (-0.5)
    shard_sum = sent_and_summed(
        jnp.dot(attended.T, upstream, preferred_element_type=jnp.float32).astype(jnp.bfloat16),
        SPACE,
        0,
    )
    gradient = over_copies(shard_sum.astype(jnp.bfloat16), "dp").astype(jnp.float32)
    return (layer, gradient * factor)


def solution(mesh):
    torus = Mesh(mesh.devices.reshape(mesh.shape["dp"], 16, 2), ("dp", "space_0", "space_1"))
    return jax.shard_map(
        shards,
        mesh=torus,
        in_specs=(
            P("dp", SPACE, None),
            P("dp", SPACE, None),
            P("dp", SPACE, None, None),
            P("dp", None),
            P("dp", SPACE, None),
            P(None, SPACE, None),
            P(),
            P(SPACE, None),
            P(SPACE, None),
            P("dp", SPACE, None),
        ),
        out_specs=(P("dp", SPACE, None), P(SPACE, None)),
        check_vma=False,
    )
```

profile of v0, /device:TPU:1, one launch (start us, length us, event | category | flops | bytes accessed | tf_op | source)
XLA Modules:
  0.0 272.7 jit_solution(14891092579451745092)
XLA Ops:
  7.2 0.0 copy-start
  7.2 0.0 all-gather.12.cloned.1.call-start
  7.3 0.7 all-gather.12.cloned.1.call-update
  8.0 0.0 all-gather.8.cloned.1.call-start
  8.0 38.3 %all-gather = bf16[112,8,512]{2,1,0:T(8,128)(2,1)} all-gather(bf16[7,8,512]{2,1,0:T(8,128)(2,1)} %param.15), channel_id=2, replica_groups=mesh['dp'=16,'space_0'=16,'space_1'=2] {'space_0'}, dimensions={0}, use_global_device_ids=true | all-gather | bytes 974848 | tf_op jit(solution)/shard_map/all_gather | solution.py:23
  46.3 0.0 all-gather.8.cloned.1.call-update
  46.3 0.0 all-gather.10.cloned.1.call-start
  46.4 30.7 %all-gather.12.cloned.1.call-done = bf16[256,2304]{1,0:T(8,128)(2,1)} async-done(((bf16[16,2304]{1,0:T(8,128)(2,1)}), bf16[256,2304]{1,0:T(8,128)(2,1)}) %all-gather.12.cloned.1.call-update) | async-done | bytes 1179664 | tf_op jit(solution)/shard_map/all_gather | solution.py:23
  77.1 0.0 all-gather.10.cloned.1.call-update
  77.1 0.7 copy.73
  77.8 18.0 %all-to-all-start = ((s32[32,1,8]{2,1,0:T(1,128)}), s32[32,1,8]{2,1,0:T(1,128)S(1)}, u32[]{:S(2)}, u32[]{:S(2)}) async-start(s32[32,1,8]{2,1,0:T(1,128)} %bitcast.2), calls=%async_computation | async-start | bytes 32768 | tf_op jit(solution)/shard_map/all_to_all | solution.py:102
  95.8 0.6 constant_dynamic-slice_fusion
  96.4 0.6 add_compare_fusion
  97.0 0.1 copy.74
  97.1 0.1 reshape.227
  97.3 0.1 reshape.235
  97.4 0.7 convert_reduce_fusion.1
  98.0 9.5 %all-to-all-done = s32[32,1,8]{2,1,0:T(1,128)S(1)} async-done(((s32[32,1,8]{2,1,0:T(1,128)}), s32[32,1,8]{2,1,0:T(1,128)S(1)}, u32[]{:S(2)}, u32[]{:S(2)}) %all-to-all-start) | async-done | bytes 1056 | tf_op jit(solution)/shard_map/all_to_all | solution.py:102
  107.6 0.1 reshape.219
  107.7 1.8 gather_fusion
  109.5 4.4 %all-to-all-start.1 = ((bf16[32,8,256]{2,1,0:T(8,128)(2,1)}), bf16[32,8,256]{2,1,0:T(8,128)(2,1)S(1)}, u32[]{:S(2)}, u32[]{:S(2)}) async-start(bf16[32,8,256]{2,1,0:T(8,128)(2,1)} %bitcast.4), calls=%async_computation.1 | async-start | bytes 262144 | tf_op jit(solution)/shard_map/all_to_all | solution.py:104
  113.9 0.6 compare_convert_fusion
  114.5 15.6 %all-to-all-done.1 = bf16[32,8,256]{2,1,0:T(8,128)(2,1)S(1)} async-done(((bf16[32,8,256]{2,1,0:T(8,128)(2,1)}), bf16[32,8,256]{2,1,0:T(8,128)(2,1)S(1)}, u32[]{:S(2)}, u32[]{:S(2)}) %all-to-all-start.1) | async-done | bytes 131104 | tf_op jit(solution)/shard_map/all_to_all | solution.py:104
  130.1 0.1 maximum_maximum_fusion
  130.2 2.7 gather_fusion.1
  132.9 0.1 reshape.226
  133.1 0.1 copy.75
  133.1 0.0 all-gather.8.cloned.1.call-done
  133.2 1.8 copy.76
  134.9 0.5 multiply_reduce_fusion
  135.5 0.0 all-gather.10.cloned.1.call-done
  135.5 0.0 copy-start.5
  135.5 1.9 copy.77
  137.4 0.5 convolution_convert_fusion
  138.0 0.2 fusion.15
  138.1 0.1 divide_convert_fusion.2
  138.2 29.0 %all-gather.3 = bf16[32,2,1536]{2,1,0:T(2,128)(2,1)S(1)} all-gather(bf16[1,2,1536]{2,1,0:T(2,128)(2,1)S(1)} %maximum_bitcast_fusion), channel_id=1, replica_groups=mesh['dp'=16,'space_0'=16,'space_1'=2] {'space_0','space_1'}, dimensions={0}, use_global_device_ids=true | all-gather | bytes 202752 | tf_op jit(solution)/shard_map/all_gather | solution.py:40
  167.2 0.1 reshape.259
  167.4 0.6 gather_fusion.2
  167.9 0.1 reshape.209
  168.0 0.3 reshape.263
  168.4 0.3 reshape.262
  168.7 0.4 fusion.30
  169.1 0.4 fusion.29
  169.6 0.7 fusion.20
  170.3 0.7 divide_convert_fusion
  171.0 0.6 gather_fusion.3
  171.6 0.1 reshape.210
  171.7 0.3 reshape.261
  172.0 0.5 fusion.11
  172.5 0.4 fusion.3
  172.9 0.4 copy.89
  173.3 0.2 convert_element_type.62
  173.5 0.3 convolution_convert_fusion.1
  173.9 52.0 %all_to_all.27 = bf16[32,24,512]{2,1,0:T(8,128)(2,1)S(1)} all-to-all(bf16[32,24,512]{2,1,0:T(8,128)(2,1)S(1)} %bitcast.70), channel_id=1, replica_groups=mesh['dp'=16,'space_0'=16,'space_1'=2] {'space_0','space_1'}, dimensions={0} | all-to-all | bytes 1572864 | tf_op jit(solution)/shard_map/all_to_all | solution.py:51
  225.8 0.1 reduce_sum.71
  226.0 0.8 broadcast_in_dim.48
  226.7 6.5 %all-to-all-start.3 = ((bf16[16,24,512]{2,1,0:T(8,128)(2,1)}), bf16[16,24,512]{2,1,0:T(8,128)(2,1)S(1)}, u32[]{:S(2)}, u32[]{:S(2)}) async-start(bf16[16,24,512]{2,1,0:T(8,128)(2,1)} %broadcast_in_dim.48), calls=%async_computation.3 | async-start | bytes 786432 | tf_op jit(solution)/shard_map/all_to_all | solution.py:57
  233.3 21.7 %all-gather.2 = bf16[384,512]{1,0:T(8,128)(2,1)S(1)} all-gather(bf16[24,512]{1,0:T(8,128)(2,1)S(1)} %copy-done.2), channel_id=4, replica_groups=mesh['dp'=16,'space_0'=16,'space_1'=2] {'space_0'}, dimensions={0}, use_global_device_ids=true | all-gather | bytes 417792 | tf_op jit(solution)/shard_map/all_gather | solution.py:23
  255.0 9.5 %all_gather.27 = bf16[32,24,512]{2,1,0:T(8,128)(2,1)S(1)} all-gather(bf16[16,24,512]{2,1,0:T(8,128)(2,1)S(1)} %bitcast.75), channel_id=1, replica_groups=mesh['dp'=16,'space_0'=16,'space_1'=2] {'space_1'}, dimensions={0}, use_global_device_ids=true | all-gather | bytes 1179648 | tf_op jit(solution)/shard_map/all_gather | solution.py:23
  264.5 0.1 copy.90
  264.6 1.0 fusion.6
  265.5 0.1 convert_reduce_fusion
  265.6 0.6 broadcast_multiply_fusion
  (28 shorter events, 0.1 us)
Async XLA Ops:
  7.2 166.3 %copy-start = (bf16[1,128,512]{2,1,0:T(8,128)(2,1)S(1)}, bf16[1,128,512]{2,1,0:T(8,128)(2,1)}, u32[]{:S(2)}) copy-start(bf16[1,128,512]{2,1,0:T(8,128)(2,1)} %param.19) | copy-start | bytes 393220
  7.2 69.9 %copy-start.3 = (s32[1,1,32,8]{2,3,1,0:T(8,128)S(1)}, s32[1,1,32,8]{2,3,1,0:T(8,128)}, u32[]{:S(2)}) copy-start(s32[1,1,32,8]{2,3,1,0:T(8,128)} %param.12) | copy-start | bytes 3076
  7.2 88.6 %copy-start.7 = (s32[1,32]{1,0:T(1,128)S(1)}, s32[1,32]{1,0:T(1,128)}, u32[]{:S(2)}) copy-start(s32[1,32]{1,0:T(1,128)} %param.13) | copy-start | bytes 388
  7.2 89.2 %copy-start.6 = (s32[1,2,4]{2,1,0:T(2,128)S(1)}, s32[1,2,4]{2,1,0:T(2,128)}, u32[]{:S(2)}) copy-start(s32[1,2,4]{2,1,0:T(2,128)} %param.14) | copy-start | bytes 100
  7.2 89.2 %copy-start.4 = (s32[1,128,6]{1,0,2:T(1,128)S(1)}, s32[1,128,6]{1,0,2:T(1,128)}, u32[]{:S(2)}) copy-start(s32[1,128,6]{1,0,2:T(1,128)} %param.11) | copy-start | bytes 9220
  7.2 100.5 %copy-start.1 = (bf16[1,128,256]{2,1,0:T(8,128)(2,1)S(1)}, bf16[1,128,256]{2,1,0:T(8,128)(2,1)}, u32[]{:S(2)}) copy-start(bf16[1,128,256]{2,1,0:T(8,128)(2,1)} %param.10) | copy-start | bytes 196612
  7.2 69.8 %all-gather.12.cloned.1.call-start = ((), (), s32[]{:S(2)}) async-start(), calls=%async_computation.6 | async-start | bytes 1253376 | tf_op jit(solution)/shard_map/all_gather | solution.py:23
  8.0 125.2 %all-gather.8.cloned.1.call-start = ((), (), s32[]{:S(2)}) async-start(), calls=%async_computation.4 | async-start | bytes 2752512 | tf_op jit(solution)/shard_map/all_gather | solution.py:23
  46.3 89.1 %all-gather.10.cloned.1.call-start = ((), (), s32[]{:S(2)}) async-start(), calls=%async_computation.5 | async-start | bytes 3538944 | tf_op jit(solution)/shard_map/all_gather | solution.py:23
  77.8 29.8 %all-to-all-start = ((s32[32,1,8]{2,1,0:T(1,128)}), s32[32,1,8]{2,1,0:T(1,128)S(1)}, u32[]{:S(2)}, u32[]{:S(2)}) async-start(s32[32,1,8]{2,1,0:T(1,128)} %bitcast.2), calls=%async_computation | async-start | bytes 32768 | tf_op jit(solution)/shard_map/all_to_all | solution.py:102
  109.5 20.6 %all-to-all-start.1 = ((bf16[32,8,256]{2,1,0:T(8,128)(2,1)}), bf16[32,8,256]{2,1,0:T(8,128)(2,1)S(1)}, u32[]{:S(2)}, u32[]{:S(2)}) async-start(bf16[32,8,256]{2,1,0:T(8,128)(2,1)} %bitcast.4), calls=%async_computation.1 | async-start | bytes 262144 | tf_op jit(solution)/shard_map/all_to_all | solution.py:104
  135.5 1.9 copy-start.5
  173.9 59.4 %copy-start.2 = (bf16[24,512]{1,0:T(8,128)(2,1)S(1)}, bf16[24,512]{1,0:T(8,128)(2,1)}, u32[]{:S(2)}) copy-start(bf16[24,512]{1,0:T(8,128)(2,1)} %param.18) | copy-start | bytes 73732
  226.7 38.8 %all-to-all-start.3 = ((bf16[16,24,512]{2,1,0:T(8,128)(2,1)}), bf16[16,24,512]{2,1,0:T(8,128)(2,1)S(1)}, u32[]{:S(2)}, u32[]{:S(2)}) async-start(bf16[16,24,512]{2,1,0:T(8,128)(2,1)} %broadcast_in_dim.48), calls=%async_computation.3 | async-start | bytes 786432 | tf_op jit(solution)/shard_map/all_to_all | solution.py:57
Sparse Core Ops, SparseCore 0:
  10.1 66.9 all-gather.11
  79.2 28.4 all-gather.7
  109.8 22.7 all-gather.9
where the time goes:
time: 273 us
  blocking collectives  150 us (55%)
  waiting for transfers between devices  56.6 us (21%)
  starting transfers between devices  29.1 us (11%)
  between operations  14.2 us (5%)
  local copies, waits for them, and re-layouts  13.9 us (5%)
  other arithmetic  4.47 us (2%)
  matrix products  4.06 us (1%)
    all_gather x3, blocking collectives, gather_in_order(): parts = lax.all_gather(parts, axes[k], axis=0, tiled=True)  69.5 us
    all_to_all x1, blocking collectives, sent_and_summed(): lax.all_to_all(parts, axis, split_axis=0, concat_axis=0, tiled=True)  52 us
    all_gather x3, waiting for transfers between devices, gather_in_order(): parts = lax.all_gather(parts, axes[k], axis=0, tiled=True)  30.7 us
    all_gather x1, blocking collectives, in_one_piece(): lax.all_gather(both, axis, axis=dim, tiled=True)  29 us
    all_to_all x1, starting transfers between devices, shards(): lax.all_to_all(wanted_rows[0, 0], SPACE, split_axis=0, concat_axis=0, til...  18 us
    all_to_all x1, waiting for transfers between devices, shards(): lax.all_to_all(answers, SPACE, split_axis=0, concat_axis=0, tiled=True)  15.6 us
    all_to_all x1, waiting for transfers between devices, shards(): lax.all_to_all(wanted_rows[0, 0], SPACE, split_axis=0, concat_axis=0, til...  9.52 us
    all_to_all x1, starting transfers between devices, sent_to_all(): return lax.all_to_all(copies, axis, split_axis=0, concat_axis=0, tiled=True)  6.53 us
  transfers between devices with their start and end apart: 6, of which 3 were waited for; matrix products, arithmetic and copies ran while one was open for 4% of the time, Pallas kernels for 0%

commit v1 on v0

v1 whole, which is shorter than its diff:
```python
import jax
import jax.numpy as jnp
from jax import lax
from jax.experimental import pallas as pl
from jax.experimental.pallas import tpu as pltpu
from jax.sharding import Mesh
from jax.sharding import PartitionSpec as P

MESH = pl.DeviceIdType.MESH
F32 = jnp.float32
BF16 = jnp.bfloat16
NZ = 16
CHUNKS = ((0, 2), (2, 4), (4, 5))


def iota(shape, dim):
    return lax.broadcasted_iota(jnp.int32, shape, dim)


def one_hot(flags):
    return jnp.where(flags, 1.0, 0.0).astype(BF16)


def ordering(parts):
    n = 256 * parts
    col = iota((1, n), 1)
    natural = ((col >> 3) & 15) * (16 * parts) + ((col >> 7) & 1) * (8 * parts) + (col >> 8) * 8 + (col & 7)
    return one_hot(iota((n, n), 0) == natural)


def dot(a, b):
    return jnp.dot(a, b, preferred_element_type=F32)


def dot_t(a, b):
    return lax.dot_general(a, b, (((1,), (1,)), ((), ())), preferred_element_type=F32)


def drain(ref, sem):
    pltpu.make_async_copy(ref, ref, sem).wait()


def kernel(
    feats, near_map, wanted, counts, choice, conv_h, gain, inw_h, outw_h, cot_h,
    layer, grad,
    asked, asks, table, answers, own_feats, taps_hot, taps, staged, held,
    hidden, qkv, tall, shorts, picked, split_q, scores, cot, att, terms, across, summed, along, final,
    order_in, order_out,
    local_sem, send_sem, recv_sem,
):
    y, x, z, c = (lax.axis_index(n) for n in ("y", "x", "z", "c"))
    other = 1 - c
    me = z * 2 + c
    plane = y * 4 + x
    a = (1 - c) * x + c * y
    b = (1 - c) * y + c * x
    piece = b * 4 + a

    def z_of(i):
        return lax.rem(z + 8 + (1 - 2 * lax.rem(i, 2)) * ((i + 1) // 2), NZ)

    def a_peer(d):
        t = lax.rem(a + d, 4)
        return t, {"x": (1 - c) * t + c * x, "y": (1 - c) * y + c * t}

    def b_peer(d):
        t = lax.rem(b + d, 4)
        return {"x": (1 - c) * x + c * t, "y": (1 - c) * t + c * y}

    def plane_peer(k):
        t = lax.rem(plane + k, 16)
        return {"y": t // 4, "x": lax.rem(t, 4)}

    def send(src, dst, s, r, where):
        pltpu.make_async_remote_copy(
            src_ref=src, dst_ref=dst, send_sem=send_sem.at[s], recv_sem=recv_sem.at[r],
            device_id=where, device_id_type=MESH,
        ).start()

    def fetch(src, dst, k):
        copy = pltpu.make_async_copy(src, dst, local_sem.at[k])
        copy.start()
        return copy

    lanes = pl.ds(pl.multiple_of(a * 128, 128), 128)
    copies = [
        fetch(cot_h.at[0], cot.at[c], 0),
        fetch(conv_h.at[2 * b, :, lanes], staged.at[0], 1),
        fetch(inw_h.at[pl.ds(0, 8), pl.ds(pl.multiple_of(piece * 128, 128), 128)], staged.at[2], 3),
        fetch(inw_h.at[pl.ds(8, 8), pl.ds(pl.multiple_of(piece * 128, 128), 128)], staged.at[3], 4),
        fetch(outw_h.at[pl.ds(pl.multiple_of(lax.rem(b, 3) * 8, 8), 8), lanes], staged.at[4], 5),
    ]

    @pl.when(b < 3)
    def _():
        fetch(conv_h.at[2 * b + 1, :, lanes], staged.at[1], 2)

    @pl.when(b == 3)
    def _():
        fetch(
            inw_h.at[pl.ds(pl.multiple_of(lax.rem(a, 2) * 8, 8), 8), pl.ds(pl.multiple_of((16 + a // 2) * 128, 128), 128)],
            staged.at[1], 2,
        )

    barrier = pltpu.get_barrier_semaphore()

    def hail(where):
        pl.semaphore_signal(barrier, inc=1, device_id=where, device_id_type=MESH)

    def hail_z(i, _):
        hail({"z": z_of(i), "c": 0})
        hail({"z": z_of(i), "c": 1})
        return 0

    lax.fori_loop(0, NZ - 1, hail_z, 0)
    lax.fori_loop(1, 16, lambda k, _: (hail(plane_peer(k)), 0)[1], 0)
    hail({"c": other})

    asks[...] = jnp.zeros_like(asks)
    for p in range(32):
        asks[p, :, 0:8] = wanted[0, 0, p : p + 1, :]
    for copy in copies:
        copy.wait()
    drain(staged.at[1], local_sem.at[2])
    held[piece, :, c, z] = staged[...]
    asked[me] = asks[me]
    ordered = dot(feats[0], ordering(1)).astype(BF16)
    own_feats[...] = ordered
    table[0:16] = ordered.reshape(16, 8, 256)
    for k in range(6):
        taps_hot[128 * k : 128 * (k + 1), :] = one_hot(near_map[0, :, k : k + 1] == iota((128, 384), 1))
    pl.semaphore_wait(barrier, 46)

    def ask(i, _):
        t = z_of(i)
        for core in range(2):
            send(asks.at[t * 2 + core], asked.at[me], 0, 0, {"z": t, "c": core})
        return 0

    lax.fori_loop(0, NZ - 1, ask, 0)
    send(asks.at[z * 2 + other], asked.at[me], 0, 0, {"c": other})
    for n, (lo, hi) in enumerate(CHUNKS):

        def spread(i, _, n=n, lo=lo, hi=hi):
            send(staged.at[lo:hi], held.at[piece, lo:hi, c, z], 1 + n, 1 + n, {"z": z_of(i)})
            return 0

        lax.fori_loop(0, NZ - 1, spread, 0)
    send(cot.at[c], cot.at[c], 4, 4, {"c": other})

    order_in[...] = ordering(2)
    order_out[...] = ordering(3)

    drain(asked.at[0:31], recv_sem.at[0])
    lists = asked[:, 0, :].astype(F32).astype(BF16)
    spread_out = dot(one_hot((iota((256, 32), 0) >> 3) == iota((256, 32), 1)), lists)
    lane = iota((256, 128), 1)
    row = jnp.sum(jnp.where(lane == (iota((256, 128), 0) & 7), spread_out, 0.0), axis=1, keepdims=True)
    picked_rows = dot(one_hot(row == lane.astype(F32)), own_feats[...]).astype(BF16)
    answers[...] = picked_rows.reshape(32, 8, 256)
    table[16 + me] = answers[me]

    def answer(i, _):
        t = z_of(i)
        for core in range(2):
            send(answers.at[t * 2 + core], table.at[16 + me], 5, 5, {"z": t, "c": core})
        return 0

    lax.fori_loop(0, NZ - 1, answer, 0)
    send(answers.at[z * 2 + other], table.at[16 + me], 5, 5, {"c": other})

    for n, (lo, hi) in enumerate(CHUNKS):
        drain(held.at[0, lo:hi, 0, 0:15], recv_sem.at[1 + n])
        for d in range(1, 4):
            part = held.at[piece, lo:hi, c]
            send(part, part, 6 + n, 6 + n, a_peer(d)[1])
    for n, (lo, hi) in enumerate(CHUNKS):
        drain(held.at[0:3, lo:hi, 0], recv_sem.at[6 + n])
        part = held.at[pl.ds(b * 4, 4), lo:hi, c]
        for d in range(1, 4):
            send(part, part, 9 + n, 9 + 3 * n + d - 1, b_peer(d))
        send(part, part, 12 + n, 18 + n, {"c": other})

    def cross(n):
        lo, hi = CHUNKS[n]
        for d in range(1, 4):
            part = held.at[pl.ds(lax.rem(b + 4 - d, 4) * 4, 4), lo:hi, c]
            drain(part, recv_sem.at[9 + 3 * n + d - 1])
            send(part, part, 12 + n, 18 + n, {"c": other})

    def crossed(n):
        lo, hi = CHUNKS[n]
        drain(held.at[:, lo:hi, 0], recv_sem.at[18 + n])

    drain(table.at[0:31], recv_sem.at[5])
    for k in range(3):
        got = dot(taps_hot[256 * k : 256 * (k + 1), :], table[...].reshape(384, 256))
        taps[2 * k : 2 * k + 2] = got.astype(BF16).reshape(2, 128, 256)
    cross(0)
    crossed(0)

    def unit(p, u):
        return held[p, u].reshape(256, 128)

    count = counts[0, me]
    alive = jnp.where(iota((128, 128), 0) < count, 1.0, 0.0)
    alive_wide = jnp.concatenate([alive, alive], axis=1)
    for t in range(0, 4, 2):
        total = jnp.zeros((128, 256), F32)
        for k in range(7):
            p, u = (k // 2) * 4 + t, k % 2
            tap = own_feats[...] if k == 0 else taps[k - 1]
            total = total + dot(tap, jnp.concatenate([unit(p, u), unit(p + 1, u)], axis=1))
        hidden[:, 128 * t : 128 * (t + 2)] = total * alive_wide
    h = hidden[...]
    power = jnp.mean(h * h, axis=-1, keepdims=True)
    normed = (h * lax.rsqrt(power + 1e-06) * gain[...]).astype(BF16)
    normed = dot(normed, order_in[...]).astype(BF16)
    cross(1)
    crossed(1)

    def project(j):
        upper, lower = [], []
        for t in (j, j + 1):
            if t < 16:
                upper.append(unit(t, 2))
                lower.append(unit(t, 3))
            else:
                upper.append(unit(12 + 2 * (t - 16), 1))
                lower.append(unit(13 + 2 * (t - 16), 1))
        got = dot(normed[:, :256], jnp.concatenate(upper, axis=1))
        got = got + dot(normed[:, 256:], jnp.concatenate(lower, axis=1))
        qkv[:, 128 * j : 128 * (j + 2)] = got.astype(BF16)

    for j in range(6, 18, 2):
        project(j)

    token = iota((8, 128), 1)
    block_mask = one_hot(((token >> 6) == iota((8, 128), 0)) & (token < count))
    sums = dot(block_mask, qkv[:, 768:])
    number = jnp.clip(count - 64 * iota((8, 1), 0), 0, 64)
    means = sums / jnp.maximum(number, 1).astype(F32)
    for j in range(12):
        tall[2 * j : 2 * j + 2, :] = means[0:2, 128 * j : 128 * (j + 1)]
    shorts[c, z] = tall[...].astype(BF16).reshape(3, 8, 128)

    def tell(i, _):
        send(shorts.at[c, z], shorts.at[c, z], 15, 21, {"z": z_of(i)})
        return 0

    lax.fori_loop(0, NZ - 1, tell, 0)

    for j in range(0, 6, 2):
        project(j)
    half = iota((128, 128), 1) < 64
    row256 = iota((256, 128), 0) & 127
    col256 = iota((256, 128), 1)
    near_ok = ((row256 >> 6) == (col256 >> 6)) & (col256 < count)
    for j in range(6):
        q = qkv[:, 128 * j : 128 * (j + 1)] * jnp.asarray(0.125, BF16)
        none = jnp.zeros_like(q)
        q = jnp.concatenate([jnp.where(half, q, none), jnp.where(half, none, q)], axis=0)
        split_q[j] = q
        scores[j] = jnp.where(near_ok, dot_t(q, qkv[:, 768 + 128 * j : 768 + 128 * (j + 1)]), -1e30)
    m96 = iota((96, 1), 0)
    target = jnp.zeros((96, 1), jnp.int32)
    for e in range(8):
        block = choice[0, e // 4, e % 4]
        shard = block // 2
        start = (lax.rem(shard, 2) * 16 + shard // 2) * 24 + lax.rem(block, 2)
        target = jnp.where((m96 & 7) == e, start, target)
    target = target + 2 * (m96 >> 3)
    chosen_hot = one_hot(target == iota((96, 768), 1))
    cross(2)

    drain(shorts.at[0, 0:15], recv_sem.at[21])
    send(shorts.at[c], shorts.at[c], 16, 22, {"c": other})
    drain(shorts.at[0], recv_sem.at[22])
    picked[...] = dot(chosen_hot, shorts[...].reshape(768, 128))
    far_ok = ((iota((256, 8), 0) & 127) >> 6) == (iota((256, 8), 1) >> 2)
    for j in range(6):
        near = scores[j]
        far = dot_t(split_q[j], picked[8 * j : 8 * j + 8, :].astype(BF16))
        far = jnp.where(far_ok, far, -1e30)
        top = jnp.maximum(jnp.max(near, axis=1, keepdims=True), jnp.max(far, axis=1, keepdims=True))
        near, far = jnp.exp(near - top), jnp.exp(far - top)
        scale = 1.0 / (jnp.sum(near, axis=1, keepdims=True) + jnp.sum(far, axis=1, keepdims=True))
        near, far = (near * scale).astype(BF16), (far * scale).astype(BF16)
        mixed = dot(near, qkv[:, 1536 + 128 * j : 1536 + 128 * (j + 1)])
        mixed = mixed + dot(far, picked[48 + 8 * j : 56 + 8 * j, :].astype(BF16))
        mixed = jnp.where(half, mixed[:128], mixed[128:]) * alive
        att[c, :, 128 * j : 128 * (j + 1)] = mixed.astype(BF16)

    send(att.at[c], att.at[c], 17, 23, {"c": other})
    drain(cot.at[0], recv_sem.at[4])
    drain(att.at[0], recv_sem.at[23])
    both = att[...].reshape(256, 768)
    for t in range(0, 4, 2):
        g = lax.dot_general(
            both, cot[:, :, 128 * t : 128 * (t + 2)].reshape(256, 256), (((0,), (0,)), ((), ())), preferred_element_type=F32
        )
        for s in range(2):
            terms[t + s] = g[:, 128 * s : 128 * (s + 1)].astype(BF16).reshape(NZ, 2, 3, 8, 128)
    for d in range(1, 4):
        t, where = a_peer(d)
        send(terms.at[t, :, c], across.at[d - 1], 18, 24, where)

    crossed(2)
    attended = dot(att[c], order_out[...]).astype(BF16)
    for t in range(0, 4, 2):
        total = hidden[:, 128 * t : 128 * (t + 2)]
        for i in range(3):
            w = jnp.concatenate([unit(4 * i + t, 4), unit(4 * i + t + 1, 4)], axis=1)
            total = total + dot(attended[:, 256 * i : 256 * (i + 1)], w)
        layer[0, :, 128 * t : 128 * (t + 2)] = total.astype(BF16)

    drain(across, recv_sem.at[24])
    total = terms[a, :, c].astype(F32)
    for d in range(3):
        total = total + across[d].astype(F32)
    summed[...] = total.astype(BF16)
    along[z] = summed[z]

    def reduce_z(i, _):
        t = z_of(i)
        send(summed.at[t], along.at[z], 19, 25, {"z": t})
        return 0

    lax.fori_loop(0, NZ - 1, reduce_z, 0)
    drain(along.at[0:15], recv_sem.at[25])
    total = along[0].astype(F32)
    for k in range(1, NZ):
        total = total + along[k].astype(F32)
    final[piece] = total.astype(BF16)

    def show(k, _):
        send(final.at[piece], final.at[piece], 20, 26, plane_peer(k))
        return 0

    lax.fori_loop(1, 16, show, 0)
    drain(final.at[0:15], recv_sem.at[26])
    factor = (16 * 4096) ** -0.5
    for t in range(4):
        total = final[t].astype(F32)
        for k in range(1, 4):
            total = total + final[4 * k + t].astype(F32)
        grad[:, 128 * t : 128 * (t + 1)] = total.reshape(24, 128) * factor

    drain(asked.at[0:31], send_sem.at[0])
    for n, (lo, hi) in enumerate(CHUNKS):
        drain(held.at[0, lo:hi, 0, 0:15], send_sem.at[1 + n])
        drain(held.at[0:3, lo:hi, 0], send_sem.at[6 + n])
        drain(held.at[0:12, lo:hi, 0], send_sem.at[9 + n])
        drain(held.at[:, lo:hi, 0], send_sem.at[12 + n])
    drain(cot.at[0], send_sem.at[4])
    drain(table.at[0:31], send_sem.at[5])
    drain(shorts.at[0, 0:15], send_sem.at[15])
    drain(shorts.at[0], send_sem.at[16])
    drain(att.at[0], send_sem.at[17])
    drain(across, send_sem.at[18])
    drain(along.at[0:15], send_sem.at[19])
    drain(final.at[0:15], send_sem.at[20])


def shards(feats, near_map, wanted, counts, choice, conv, gain, inw, outw, cot):
    vmem = pl.BlockSpec(memory_space=pltpu.VMEM)
    smem = pl.BlockSpec(memory_space=pltpu.SMEM)
    anywhere = pl.BlockSpec(memory_space=pl.ANY)
    v = pltpu.VMEM
    return pl.pallas_call(
        kernel,
        name="layer",
        out_shape=(jax.ShapeDtypeStruct((1, 128, 512), BF16), jax.ShapeDtypeStruct((24, 512), F32)),
        in_specs=[vmem, vmem, vmem, smem, smem, anywhere, vmem, anywhere, anywhere, anywhere],
        out_specs=(vmem, vmem),
        scratch_shapes=[
            v((32, 1, 128), jnp.int32),
            v((32, 1, 128), jnp.int32),
            v((48, 8, 256), BF16),
            v((32, 8, 256), BF16),
            v((128, 256), BF16),
            v((768, 384), BF16),
            v((6, 128, 256), BF16),
            v((5, 8, 128), BF16),
            v((16, 5, 2, NZ, 8, 128), BF16),
            v((128, 512), F32),
            v((128, 2304), BF16),
            v((24, 128), F32),
            v((2, NZ, 3, 8, 128), BF16),
            v((96, 128), F32),
            v((6, 256, 128), BF16),
            v((6, 256, 128), F32),
            v((2, 128, 512), BF16),
            v((2, 128, 768), BF16),
            v((4, NZ, 2, 3, 8, 128), BF16),
            v((3, NZ, 3, 8, 128), BF16),
            v((NZ, 3, 8, 128), BF16),
            v((NZ, 3, 8, 128), BF16),
            v((16, 3, 8, 128), BF16),
            v((512, 512), BF16),
            v((768, 768), BF16),
            pltpu.SemaphoreType.DMA((6,)),
            pltpu.SemaphoreType.DMA((21,)),
            pltpu.SemaphoreType.DMA((27,)),
        ],
        compiler_params=pltpu.CompilerParams(
            collective_id=0, has_side_effects=True, vmem_limit_bytes=48 * 1024 * 1024
        ),
    )(feats, near_map, wanted, counts, choice, conv, gain.reshape(1, -1), inw, outw, cot)


def solution(mesh):
    space = ("z", "c")
    dp = ("y", "x")
    torus = Mesh(mesh.devices.reshape(4, 4, 16, 2), dp + space)
    return jax.shard_map(
        shards,
        mesh=torus,
        in_specs=(
            P(dp, space, None),
            P(dp, space, None),
            P(dp, space, None, None),
            P(dp, None),
            P(dp, space, None),
            P(None, space, None),
            P(),
            P(space, None),
            P(space, None),
            P(dp, space, None),
        ),
        out_specs=(P(dp, space, None), P(space, None)),
        check_vma=False,
    )
```

time: 273 us -> 83.7 us (0.31)
  blocking collectives: 150 us -> 0 us
  Pallas kernels: 0 us -> 76.4 us
  waiting for transfers between devices: 56.6 us -> 0 us
  starting transfers between devices: 29.1 us -> 0 us
  between operations: 14.2 us -> 0.69 us
  local copies, waits for them, and re-layouts: 13.9 us -> 6.21 us
  other arithmetic: 4.47 us -> 0 us
  matrix products: 4.06 us -> 0 us
    all_gather x4 -> x0, blocking collectives: 98.5 us -> none  [the longest x3 69.5 us: gather_in_order(): parts = lax.all_gather(parts, axes[k], axis=0, tiled=True)]
    pallas_call x0 -> x1, Pallas kernels: none -> 76.4 us  [shards(): pl.pallas_call(kernel, name='layer', out_shape=(jax.ShapeDtypeStruct((1,...]
    all_to_all x1 -> x0, blocking collectives: 52 us -> none  [sent_and_summed(): lax.all_to_all(parts, axis, split_axis=0, concat_axis=0, tiled=True)]
    all_gather x3 -> x0, waiting for transfers between devices: 30.7 us -> none  [gather_in_order(): parts = lax.all_gather(parts, axes[k], axis=0, tiled=True)]
    all_to_all x3 -> x0, starting transfers between devices: 29 us -> none  [the longest x1 18 us: shards(): lax.all_to_all(wanted_rows[0, 0], SPACE, split_axis=0, concat_axis=0, til...]
    all_to_all x3 -> x0, waiting for transfers between devices: 25.1 us -> none  [the longest x1 15.6 us: shards(): lax.all_to_all(answers, SPACE, split_axis=0, concat_axis=0, tiled=True)]
    gather x6 -> x0, local copies, waits for them, and re-layouts: 5.81 us -> none  [the longest x3 2.86 us: shards(): gathered_taps = padded[index_map]]
    unnamed x18 -> x20, local copies, waits for them, and re-layouts: 0.8 us -> 6.21 us
  transfers between devices with their start and end apart: 6 -> 0, of which waited for: 3 -> 0; matrix products, arithmetic and copies ran while one was open for 4% -> 0% of each run, Pallas kernels for 0% -> 0%
where the time goes in v1:
time: 83.7 us; the launch traced here: 83.3 us
  Pallas kernels  76.4 us (91%)
  local copies, waits for them, and re-layouts  6.21 us (7%)
    pallas_call x1, Pallas kernels, shards(): pl.pallas_call(kernel, name='layer', out_shape=(jax.ShapeDtypeStruct((1,...  76.4 us
    unnamed x20, local copies, waits for them, and re-layouts  6.21 us

profile of v1, /device:TPU:1, one launch (start us, length us, event | category | flops | bytes accessed | tf_op | source)
XLA Modules:
  0.0 83.3 jit_solution(7553652861274573419)
XLA Ops:
  0.6 0.0 copy-start.1
  0.6 0.8 copy.13.wanted
  1.4 0.0 copy-start.5
  1.4 0.0 copy-start.6
  1.4 0.0 copy-start.7
  1.4 0.8 copy.12.near_map
  2.3 0.0 copy-done.1
  2.3 0.0 copy-done.5
  2.3 0.0 copy-done.6
  2.3 0.0 copy-done.7
  2.3 0.0 copy-start
  2.3 0.9 %copy-done = bf16[1,128,512]{2,1,0:T(8,128)(2,1)S(1)} copy-done((bf16[1,128,512]{2,1,0:T(8,128)(2,1)S(1)}, bf16[1,128,512]{2,1,0:T(8,128)(2,1)}, u32[]{:S(2)}) %copy-start) | copy-done | bytes 131096
  3.2 0.0 copy-start.2
  3.2 0.8 %copy-done.2 = bf16[1,128,256]{2,1,0:T(8,128)(2,1)S(1)} copy-done((bf16[1,128,256]{2,1,0:T(8,128)(2,1)S(1)}, bf16[1,128,256]{2,1,0:T(8,128)(2,1)}, u32[]{:S(2)}) %copy-start.2) | copy-done | bytes 65560
  4.1 0.0 copy-start.3
  4.1 0.8 copy-done.3
  4.9 0.0 copy-start.4
  4.9 0.7 copy-done.4
  5.6 76.4 %layer.1 = (bf16[1,128,512]{2,1,0:T(8,128)(2,1)S(1)}, f32[24,512]{1,0:T(8,128)S(1)}) custom-call(bf16[1,128,256]{2,1,0:T(8,128)(2,1)S(1)} %copy-done.2, s32[1,128,6]{2,1,0:T(8,128)S(1)} %copy.12.near_map, s32[1,1,32,8]{3,2,1,0:T(8,128)S(1)} %copy.13.wanted, s32[1,32]{1,0:T(1,128)S(1)} %copy-done.7, s32[1,2,4]{2,1,0:T(2,128)S(1)} %copy-done.6, ...), custom_call_target="tpu_custom_call" | custom-call | tf_op jit(solution)/shard_map/layer/pallas_call | solution.py:370
  82.1 0.7 copy.16
  82.7 0.6 copy.17
Async XLA Ops:
  0.6 1.6 %copy-start.1 = (bf16[16,2304]{1,0:T(8,128)(2,1)S(1)}, bf16[16,2304]{1,0:T(8,128)(2,1)}, u32[]{:S(2)}) copy-start(bf16[16,2304]{1,0:T(8,128)(2,1)} %inw_h.1) | copy-start | bytes 221188
  1.4 0.8 %copy-start.5 = (f32[512]{0:T(512)S(1)}, f32[512]{0:T(512)}, u32[]{:S(2)}) copy-start(f32[512]{0:T(512)} %param.16) | copy-start | bytes 6148
  1.4 0.9 %copy-start.6 = (s32[1,2,4]{2,1,0:T(2,128)S(1)}, s32[1,2,4]{2,1,0:T(2,128)}, u32[]{:S(2)}) copy-start(s32[1,2,4]{2,1,0:T(2,128)} %choice.1) | copy-start | bytes 100
  1.4 0.9 %copy-start.7 = (s32[1,32]{1,0:T(1,128)S(1)}, s32[1,32]{1,0:T(1,128)}, u32[]{:S(2)}) copy-start(s32[1,32]{1,0:T(1,128)} %counts.1) | copy-start | bytes 388
  2.3 0.9 %copy-start = (bf16[1,128,512]{2,1,0:T(8,128)(2,1)S(1)}, bf16[1,128,512]{2,1,0:T(8,128)(2,1)}, u32[]{:S(2)}) copy-start(bf16[1,128,512]{2,1,0:T(8,128)(2,1)} %cot_h.1) | copy-start | bytes 393220
  3.2 0.8 %copy-start.2 = (bf16[1,128,256]{2,1,0:T(8,128)(2,1)S(1)}, bf16[1,128,256]{2,1,0:T(8,128)(2,1)}, u32[]{:S(2)}) copy-start(bf16[1,128,256]{2,1,0:T(8,128)(2,1)} %feats.1) | copy-start | bytes 196612
  4.1 0.8 copy-start.3
  4.9 0.7 copy-start.4

commit v2 on v1

v2 whole, which is shorter than its diff:
```python
import jax
import jax.numpy as jnp
from jax import lax
from jax.experimental import pallas as pl
from jax.experimental.pallas import tpu as pltpu
from jax.sharding import Mesh
from jax.sharding import PartitionSpec as P

MESH = pl.DeviceIdType.MESH
F32 = jnp.float32
BF16 = jnp.bfloat16
NZ = 16
VMEM = 48 * 1024 * 1024
CHUNKS = ((0, 2, 0, 8), (0, 2, 8, 16), (2, 4, 0, 8), (2, 4, 8, 16), (4, 5, 0, 16))


def iota(shape, dim):
    return lax.broadcasted_iota(jnp.int32, shape, dim)


def one_hot(flags):
    return jnp.where(flags, 1.0, 0.0).astype(BF16)


def ordering(parts, z):
    n = 256 * parts
    col = iota((1, n), 1)
    slot = (col >> 3) & 15
    chip = (z + NZ + jnp.where((slot & 1) == 1, (slot + 1) >> 1, -(slot >> 1))) & 15
    natural = chip * (16 * parts) + ((col >> 7) & 1) * (8 * parts) + (col >> 8) * 8 + (col & 7)
    return one_hot(iota((n, n), 0) == natural)


def dot(a, b):
    return jnp.dot(a, b, preferred_element_type=F32)


def dot_t(a, b):
    return lax.dot_general(a, b, (((1,), (1,)), ((), ())), preferred_element_type=F32)


def drain(ref, sem):
    pltpu.make_async_copy(ref, ref, sem).wait()


def kernel(
    feats_h, near_h, wanted_h, counts_h, choice_h, conv_h, gain_h, inw_h, outw_h, cot_h,
    layer, grad,
    feats, near_map, wanted, counts, choice, gain, turned,
    asked, asks, table, answers, own_feats, taps_hot, taps, staged, held,
    hidden, qkv, tall, shorts, picked, split_q, scores, cot, att, terms, across, summed, along, final,
    order_taps, order_in, order_out,
    local_sem, send_sem, recv_sem,
):
    y, x, z, c = (lax.axis_index(n) for n in ("y", "x", "z", "c"))
    other = 1 - c
    me = z * 2 + c
    plane = y * 4 + x
    a = (1 - c) * x + c * y
    b = (1 - c) * y + c * x
    piece = b * 4 + a

    def z_of(slot):
        return lax.rem(z + NZ - (2 * lax.rem(slot, 2) - 1) * ((slot + 1) // 2), NZ)

    def a_peer(d):
        t = lax.rem(a + d, 4)
        return t, {"x": (1 - c) * t + c * x, "y": (1 - c) * y + c * t}

    def b_peer(d):
        t = lax.rem(b + d, 4)
        return t, {"x": (1 - c) * x + c * t, "y": (1 - c) * t + c * y}

    def plane_peer(k):
        t = lax.rem(plane + k, 16)
        return {"y": t // 4, "x": lax.rem(t, 4)}

    def send(src, dst, s, r, where):
        pltpu.make_async_remote_copy(
            src_ref=src, dst_ref=dst, send_sem=send_sem.at[s], recv_sem=recv_sem.at[r],
            device_id=where, device_id_type=MESH,
        ).start()

    def fetch(src, dst, k):
        copy = pltpu.make_async_copy(src, dst, local_sem.at[k])
        copy.start()
        return copy

    lanes = pl.ds(pl.multiple_of(a * 128, 128), 128)
    first = [
        fetch(wanted_h, wanted, 6),
        fetch(near_h, near_map, 7),
        fetch(feats_h.at[0], feats, 8),
    ]
    later = [
        fetch(counts_h, counts, 9),
        fetch(choice_h, choice, 10),
        fetch(gain_h, gain, 11),
    ]
    copies = [
        fetch(cot_h.at[0], cot.at[c], 0),
        fetch(conv_h.at[2 * b, :, lanes], staged.at[0], 1),
        fetch(inw_h.at[pl.ds(0, 8), pl.ds(pl.multiple_of(piece * 128, 128), 128)], staged.at[2], 3),
        fetch(inw_h.at[pl.ds(8, 8), pl.ds(pl.multiple_of(piece * 128, 128), 128)], staged.at[3], 4),
        fetch(outw_h.at[pl.ds(pl.multiple_of(lax.rem(b, 3) * 8, 8), 8), lanes], staged.at[4], 5),
    ]

    @pl.when(b < 3)
    def _():
        fetch(conv_h.at[2 * b + 1, :, lanes], staged.at[1], 2)

    @pl.when(b == 3)
    def _():
        fetch(
            inw_h.at[pl.ds(pl.multiple_of(lax.rem(a, 2) * 8, 8), 8), pl.ds(pl.multiple_of((16 + a // 2) * 128, 128), 128)],
            staged.at[1], 2,
        )

    barrier = pltpu.get_barrier_semaphore()

    def hail(where):
        pl.semaphore_signal(barrier, inc=1, device_id=where, device_id_type=MESH)

    def hail_z(i, _):
        hail({"z": z_of(i), "c": 0})
        hail({"z": z_of(i), "c": 1})
        return 0

    lax.fori_loop(1, NZ, hail_z, 0)
    lax.fori_loop(1, 16, lambda k, _: (hail(plane_peer(k)), 0)[1], 0)
    hail({"c": other})

    turned[...] = jnp.zeros_like(turned)
    for copy in first:
        copy.wait()
    turned[0, 0:8, 0:32] = wanted[0, 0].astype(F32)
    for k in range(6):
        turned[1, k : k + 1, :] = near_map[k].astype(F32)
    lists = turned[0].T.astype(jnp.int32)
    for p in range(32):
        asks[p] = lists[p : p + 1, :]
    asked[me] = asks[me]
    rows = turned[1].T
    for k in range(6):
        taps_hot[128 * k : 128 * (k + 1), :] = one_hot(rows[:, k : k + 1].astype(jnp.int32) == iota((128, 384), 1))
    order_taps[...] = ordering(1, z)
    ordered = dot(feats[...], order_taps[...]).astype(BF16)
    own_feats[...] = ordered
    table[0:16] = ordered.reshape(16, 8, 256)
    for copy in copies:
        copy.wait()
    drain(staged.at[1], local_sem.at[2])
    held[piece, :, c, 0] = staged[...]
    with jax.named_scope("w_barrier"):
        pl.semaphore_wait(barrier, 46)

    def far_first(body):
        lax.fori_loop(1, NZ, lambda i, _: (body(NZ - i), 0)[1], 0)

    def ask(slot):
        t = z_of(slot)
        for core in range(2):
            send(asks.at[t * 2 + core], asked.at[me], 0, 0, {"z": t, "c": core})

    def spread(n):
        lo, hi, s0, s1 = CHUNKS[n]

        def one(slot, _):
            send(staged.at[lo:hi], held.at[piece, lo:hi, c, slot], 5 + n, 7 + n, {"z": z_of(slot)})
            return 0

        lax.fori_loop(max(s0, 1), s1, one, 0)

    far_first(ask)
    send(asks.at[z * 2 + other], asked.at[me], 0, 0, {"c": other})
    for n in range(4):
        spread(n)
    send(cot.at[c], cot.at[c], 1, 1, {"c": other})
    for copy in later:
        copy.wait()
    order_in[...] = ordering(2, z)
    order_out[...] = ordering(3, z)

    def part(n, p, count, from_slot=None, to_slot=None):
        lo, hi, s0, s1 = CHUNKS[n]
        return held.at[pl.ds(p, count), lo:hi, c, s0 if from_slot is None else from_slot : s1 if to_slot is None else to_slot]

    def cross(n, p, count, *slots):
        some = part(n, p, count, *slots)
        send(some, some, 20 + n, 32 + n, {"c": other})

    def along_a(n):
        lo, hi, s0, s1 = CHUNKS[n]
        with jax.named_scope(f"w_z{n}"):
            drain(held.at[0, lo:hi, 0, max(s0, 1) : s1], recv_sem.at[7 + n])
        for d in (2, 1, 3):
            send(part(n, piece, 1), part(n, piece, 1), 10 + n, 12 + n, a_peer(d)[1])

    def along_b(n):
        lo, hi, s0, s1 = CHUNKS[n]
        with jax.named_scope(f"w_a{n}"):
            drain(held.at[0:3, lo:hi, 0, s0:s1], recv_sem.at[12 + n])
        for k, d in enumerate((1, 3)):
            send(part(n, b * 4, 4), part(n, b * 4, 4), 15 + n, 17 + 5 * k + n, b_peer(d)[1])
        cross(n, b * 4, 4)

    def relay(n):
        lo, hi, s0, s1 = CHUNKS[n]
        middle = (s0 + s1) // 2
        for k, d, low, high in ((0, 1, s0, middle), (1, 3, middle, s1)):
            source = lax.rem(b + 4 - d, 4) * 4
            with jax.named_scope(f"w_b{n}"):
                drain(part(n, source, 4), recv_sem.at[17 + 5 * k + n])
            send(part(n, source, 4, low, high), part(n, source, 4, low, high), 15 + n, 27 + n, b_peer(d)[1])
            cross(n, source, 4)

    def last(n):
        source = lax.rem(b + 2, 4) * 4
        with jax.named_scope(f"w_f{n}"):
            drain(part(n, source, 4), recv_sem.at[27 + n])
        cross(n, source, 4)

    def crossed(n):
        lo, hi, s0, s1 = CHUNKS[n]
        with jax.named_scope(f"w_c{n}"):
            drain(held.at[:, lo:hi, 0, s0:s1], recv_sem.at[32 + n])

    along_a(0)

    with jax.named_scope("w_ask"):
        drain(asked.at[0:31], recv_sem.at[0])
    lists = asked[:, 0, :].astype(F32).astype(BF16)
    spread_out = dot(one_hot((iota((256, 32), 0) >> 3) == iota((256, 32), 1)), lists)
    lane = iota((256, 128), 1)
    row = jnp.sum(jnp.where(lane == (iota((256, 128), 0) & 7), spread_out, 0.0), axis=1, keepdims=True)
    picked_rows = dot(one_hot(row == lane.astype(F32)), feats[...]).astype(BF16)
    answers[...] = picked_rows.reshape(32, 8, 256)
    table[16 + me] = answers[me]

    def answer(slot):
        t = z_of(slot)
        for core in range(2):
            send(answers.at[t * 2 + core], table.at[16 + me], 2, 2, {"z": t, "c": core})

    far_first(answer)
    send(answers.at[z * 2 + other], table.at[16 + me], 2, 2, {"c": other})
    spread(4)

    along_b(0)
    along_a(1)
    along_a(2)
    relay(0)
    along_b(1)
    along_a(3)
    along_b(2)
    relay(1)
    last(0)
    along_b(3)
    relay(2)
    last(1)
    with jax.named_scope("w_rows"):
        drain(table.at[0:31], recv_sem.at[2])
    fetched = table[16:48].reshape(256, 256)
    table[16:48] = dot(fetched, order_taps[...]).astype(BF16).reshape(32, 8, 256)
    for k in range(3):
        got = dot(taps_hot[256 * k : 256 * (k + 1), :], table[...].reshape(384, 256))
        taps[2 * k : 2 * k + 2] = got.astype(BF16).reshape(2, 128, 256)
    relay(3)
    last(2)
    crossed(0)
    crossed(1)

    def unit(p, u):
        return held[p, u].reshape(256, 128)

    count = counts[0, me]
    alive = jnp.where(iota((128, 128), 0) < count, 1.0, 0.0)
    alive_wide = jnp.concatenate([alive, alive], axis=1)
    for t in range(0, 4, 2):
        total = jnp.zeros((128, 256), F32)
        for k in range(7):
            p, u = (k // 2) * 4 + t, k % 2
            tap = own_feats[...] if k == 0 else taps[k - 1]
            total = total + dot(tap, jnp.concatenate([unit(p, u), unit(p + 1, u)], axis=1))
        hidden[:, 128 * t : 128 * (t + 2)] = total * alive_wide
    h = hidden[...]
    power = jnp.mean(h * h, axis=-1, keepdims=True)
    normed = (h * lax.rsqrt(power + 1e-06) * gain[...]).astype(BF16)
    normed = dot(normed, order_in[...]).astype(BF16)
    last(3)
    crossed(2)
    crossed(3)

    def project(j):
        upper, lower = [], []
        for t in (j, j + 1):
            if t < 16:
                upper.append(unit(t, 2))
                lower.append(unit(t, 3))
            else:
                upper.append(unit(12 + 2 * (t - 16), 1))
                lower.append(unit(13 + 2 * (t - 16), 1))
        got = dot(normed[:, :256], jnp.concatenate(upper, axis=1))
        got = got + dot(normed[:, 256:], jnp.concatenate(lower, axis=1))
        qkv[:, 128 * j : 128 * (j + 2)] = got.astype(BF16)

    for j in range(6, 18, 2):
        project(j)

    token = iota((8, 128), 1)
    block_mask = one_hot(((token >> 6) == iota((8, 128), 0)) & (token < count))
    sums = dot(block_mask, qkv[:, 768:])
    number = jnp.clip(count - 64 * iota((8, 1), 0), 0, 64)
    means = sums / jnp.maximum(number, 1).astype(F32)
    for j in range(12):
        tall[2 * j : 2 * j + 2, :] = means[0:2, 128 * j : 128 * (j + 1)]
    shorts[c, z] = tall[...].astype(BF16).reshape(3, 8, 128)

    far_first(lambda slot: send(shorts.at[c, z], shorts.at[c, z], 3, 3, {"z": z_of(slot)}))
    along_a(4)

    for j in range(0, 6, 2):
        project(j)
    half = iota((128, 128), 1) < 64
    row256 = iota((256, 128), 0) & 127
    col256 = iota((256, 128), 1)
    near_ok = ((row256 >> 6) == (col256 >> 6)) & (col256 < count)
    for j in range(6):
        q = qkv[:, 128 * j : 128 * (j + 1)] * jnp.asarray(0.125, BF16)
        none = jnp.zeros_like(q)
        q = jnp.concatenate([jnp.where(half, q, none), jnp.where(half, none, q)], axis=0)
        split_q[j] = q
        scores[j] = jnp.where(near_ok, dot_t(q, qkv[:, 768 + 128 * j : 768 + 128 * (j + 1)]), -1e30)
    m96 = iota((96, 1), 0)
    target = jnp.zeros((96, 1), jnp.int32)
    for e in range(8):
        block = choice[0, e // 4, e % 4]
        shard = block // 2
        start = (lax.rem(shard, 2) * 16 + shard // 2) * 24 + lax.rem(block, 2)
        target = jnp.where((m96 & 7) == e, start, target)
    target = target + 2 * (m96 >> 3)
    chosen_hot = one_hot(target == iota((96, 768), 1))
    along_b(4)
    relay(4)
    last(4)

    with jax.named_scope("w_short"):
        drain(shorts.at[0, 0:15], recv_sem.at[3])
    send(shorts.at[c], shorts.at[c], 4, 4, {"c": other})
    with jax.named_scope("w_shortc"):
        drain(shorts.at[0], recv_sem.at[4])
    picked[...] = dot(chosen_hot, shorts[...].reshape(768, 128))
    far_ok = ((iota((256, 8), 0) & 127) >> 6) == (iota((256, 8), 1) >> 2)
    for j in range(6):
        near = scores[j]
        far = dot_t(split_q[j], picked[8 * j : 8 * j + 8, :].astype(BF16))
        far = jnp.where(far_ok, far, -1e30)
        top = jnp.maximum(jnp.max(near, axis=1, keepdims=True), jnp.max(far, axis=1, keepdims=True))
        near, far = jnp.exp(near - top), jnp.exp(far - top)
        scale = 1.0 / (jnp.sum(near, axis=1, keepdims=True) + jnp.sum(far, axis=1, keepdims=True))
        near, far = (near * scale).astype(BF16), (far * scale).astype(BF16)
        mixed = dot(near, qkv[:, 1536 + 128 * j : 1536 + 128 * (j + 1)])
        mixed = mixed + dot(far, picked[48 + 8 * j : 56 + 8 * j, :].astype(BF16))
        mixed = jnp.where(half, mixed[:128], mixed[128:]) * alive
        att[c, :, 128 * j : 128 * (j + 1)] = mixed.astype(BF16)
        if j % 3 == 2:
            part_of = att.at[c, :, 128 * (j - 2) : 128 * (j + 1)]
            send(part_of, part_of, 25 + j // 3, 5 + j // 3, {"c": other})

    drain(cot.at[0], recv_sem.at[1])
    for g in range(2):
        cols, rows = slice(384 * g, 384 * (g + 1)), slice(8 * g, 8 * (g + 1))
        with jax.named_scope(f"w_att{g}"):
            drain(att.at[0, :, cols], recv_sem.at[5 + g])
        both = att[:, :, cols].reshape(256, 384)
        for t in range(0, 4, 2):
            got = lax.dot_general(
                both, cot[:, :, 128 * t : 128 * (t + 2)].reshape(256, 256), (((0,), (0,)), ((), ())),
                preferred_element_type=F32,
            )
            for k in range(2):
                terms[t + k, rows] = got[:, 128 * k : 128 * (k + 1)].astype(BF16).reshape(8, 2, 3, 8, 128)
        for d in (2, 1, 3):
            t, where = a_peer(d)
            send(terms.at[t, rows, c], across.at[d - 1, rows], 27 + g, 37 + g, where)

    crossed(4)
    attended = dot(att[c], order_out[...]).astype(BF16)
    for t in range(0, 4, 2):
        total = hidden[:, 128 * t : 128 * (t + 2)]
        for i in range(3):
            w = jnp.concatenate([unit(4 * i + t, 4), unit(4 * i + t + 1, 4)], axis=1)
            total = total + dot(attended[:, 256 * i : 256 * (i + 1)], w)
        layer[0, :, 128 * t : 128 * (t + 2)] = total.astype(BF16)

    for g in range(2):
        rows = slice(8 * g, 8 * (g + 1))
        with jax.named_scope(f"w_across{g}"):
            drain(across.at[:, rows], recv_sem.at[37 + g])
        total = terms[a, rows, c].astype(F32)
        for d in range(3):
            total = total + across[d, rows].astype(F32)
        summed[rows] = total.astype(BF16)

        def reduce_z(t, _):
            @pl.when(t != z)
            def _():
                send(summed.at[t], along.at[z], 29, 39, {"z": t})

            return 0

        lax.fori_loop(8 * g, 8 * (g + 1), reduce_z, 0)
    along[z] = summed[z]
    with jax.named_scope("w_along"):
        drain(along.at[0:15], recv_sem.at[39])
    total = along[0].astype(F32)
    for k in range(1, NZ):
        total = total + along[k].astype(F32)
    final[piece] = total.astype(BF16)

    def show(k, _):
        send(final.at[piece], final.at[piece], 30, 40, plane_peer(k))
        return 0

    lax.fori_loop(1, 16, show, 0)
    with jax.named_scope("w_final"):
        drain(final.at[0:15], recv_sem.at[40])
    factor = (16 * 4096) ** -0.5
    for t in range(4):
        total = final[t].astype(F32)
        for k in range(1, 4):
            total = total + final[4 * k + t].astype(F32)
        grad[:, 128 * t : 128 * (t + 1)] = total.reshape(24, 128) * factor

    drain(asked.at[0:31], send_sem.at[0])
    drain(cot.at[0], send_sem.at[1])
    drain(table.at[0:31], send_sem.at[2])
    drain(shorts.at[0, 0:15], send_sem.at[3])
    drain(shorts.at[0], send_sem.at[4])
    for n, (lo, hi, s0, s1) in enumerate(CHUNKS):
        drain(held.at[0, lo:hi, 0, max(s0, 1) : s1], send_sem.at[5 + n])
        drain(held.at[0:3, lo:hi, 0, s0:s1], send_sem.at[10 + n])
        drain(held.at[0:12, lo:hi, 0, s0:s1], send_sem.at[15 + n])
        drain(held.at[:, lo:hi, 0, s0:s1], send_sem.at[20 + n])
    for g in range(2):
        drain(att.at[0, :, 384 * g : 384 * (g + 1)], send_sem.at[25 + g])
        drain(across.at[:, 8 * g : 8 * (g + 1)], send_sem.at[27 + g])
    drain(along.at[0:15], send_sem.at[29])
    drain(final.at[0:15], send_sem.at[30])


def shards(feats, near_map, wanted, counts, choice, conv, gain, inw, outw, cot):
    vmem = pl.BlockSpec(memory_space=pltpu.VMEM)
    hbm = pl.BlockSpec(memory_space=pltpu.HBM)
    v = pltpu.VMEM
    return pl.pallas_call(
        kernel,
        name="layer",
        out_shape=(jax.ShapeDtypeStruct((1, 128, 512), BF16), jax.ShapeDtypeStruct((24, 512), F32)),
        in_specs=[hbm] * 10,
        out_specs=(vmem, vmem),
        scratch_shapes=[
            v((128, 256), BF16),
            v((6, 1, 128), jnp.int32),
            v((1, 1, 8, 32), jnp.int32),
            pltpu.SMEM((1, 32), jnp.int32),
            pltpu.SMEM((1, 2, 4), jnp.int32),
            v((1, 512), F32),
            v((2, 128, 128), F32),
            v((32, 1, 128), jnp.int32),
            v((32, 1, 128), jnp.int32),
            v((48, 8, 256), BF16),
            v((32, 8, 256), BF16),
            v((128, 256), BF16),
            v((768, 384), BF16),
            v((6, 128, 256), BF16),
            v((5, 8, 128), BF16),
            v((16, 5, 2, NZ, 8, 128), BF16),
            v((128, 512), F32),
            v((128, 2304), BF16),
            v((24, 128), F32),
            v((2, NZ, 3, 8, 128), BF16),
            v((96, 128), F32),
            v((6, 256, 128), BF16),
            v((6, 256, 128), F32),
            v((2, 128, 512), BF16),
            v((2, 128, 768), BF16),
            v((4, NZ, 2, 3, 8, 128), BF16),
            v((3, NZ, 3, 8, 128), BF16),
            v((NZ, 3, 8, 128), BF16),
            v((NZ, 3, 8, 128), BF16),
            v((16, 3, 8, 128), BF16),
            v((256, 256), BF16),
            v((512, 512), BF16),
            v((768, 768), BF16),
            pltpu.SemaphoreType.DMA((12,)),
            pltpu.SemaphoreType.DMA((31,)),
            pltpu.SemaphoreType.DMA((41,)),
        ],
        compiler_params=pltpu.CompilerParams(
            collective_id=0, has_side_effects=True, vmem_limit_bytes=VMEM
        ),
    )(
        *(
            pltpu.with_memory_space_constraint(array, pltpu.HBM)
            for array in (
                feats, near_map.transpose(2, 0, 1), wanted.swapaxes(2, 3), counts, choice, conv, gain.reshape(1, -1), inw, outw, cot
            )
        )
    )


def solution(mesh):
    space = ("z", "c")
    dp = ("y", "x")
    torus = Mesh(mesh.devices.reshape(4, 4, 16, 2), dp + space)
    return jax.shard_map(
        shards,
        mesh=torus,
        in_specs=(
            P(dp, space, None),
            P(dp, space, None),
            P(dp, space, None, None),
            P(dp, None),
            P(dp, space, None),
            P(None, space, None),
            P(),
            P(space, None),
            P(space, None),
            P(dp, space, None),
        ),
        out_specs=(P(dp, space, None), P(space, None)),
        check_vma=False,
    )
```

time: 83.7 us -> 80.2 us (0.958)
  local copies, waits for them, and re-layouts: 6.21 us -> 1.28 us
  Pallas kernels: 76.4 us -> 77.5 us
    unnamed x20 -> x2, local copies, waits for them, and re-layouts: 6.21 us -> 1.28 us
    pallas_call x1, Pallas kernels: 76.4 us -> 77.5 us  [shards(): pl.pallas_call(kernel, name='layer', out_shape=(jax.ShapeDtypeStruct((1,...]
where the time goes in v2:
time: 80.2 us; the launch traced here: 79.5 us
  Pallas kernels  77.5 us (97%)
  local copies, waits for them, and re-layouts  1.28 us (2%)
    pallas_call x1, Pallas kernels, shards(): pl.pallas_call(kernel, name='layer', out_shape=(jax.ShapeDtypeStruct((1,...  77.5 us

profile of v2, /device:TPU:1, one launch (start us, length us, event | category | flops | bytes accessed | tf_op | source)
XLA Modules:
  0.0 79.5 jit_solution(16357817916342034340)
XLA Ops:
  0.6 77.5 %layer.1 = (bf16[1,128,512]{2,1,0:T(8,128)(2,1)S(1)}, f32[24,512]{1,0:T(8,128)S(1)}) custom-call(bf16[1,128,256]{2,1,0:T(8,128)(2,1)} %feats_h.1, s32[6,1,128]{2,1,0:T(1,128)} %bitcast.4, s32[1,1,8,32]{3,2,1,0:T(8,128)} %bitcast.3, s32[1,32]{1,0:T(1,128)} %counts_h.1, s32[1,2,4]{2,1,0:T(2,128)} %choice_h.1, bf16[7,8,512]{2,1,0:T(8,128)(2,1)} %conv_h.1, ...), custom_call_target="tpu_custom_call" | custom-call | tf_op jit(solution)/shard_map/layer/pallas_call | solution.py:456
  78.2 0.7 copy.14
  78.8 0.6 copy.15

commit v3 on v2

--- a/solution.py
+++ b/solution.py
@@ -11,7 +11,10 @@
 BF16 = jnp.bfloat16
 NZ = 16
 VMEM = 48 * 1024 * 1024
-CHUNKS = ((0, 2, 0, 8), (0, 2, 8, 16), (2, 4, 0, 8), (2, 4, 8, 16), (4, 5, 0, 16))
+CHUNKS = (
+    (0, 2, 0, 8, 0), (0, 2, 8, 16, 0), (0, 2, 0, 8, 1), (0, 2, 8, 16, 1), (2, 4, 0, 16, 0), (2, 4, 0, 16, 1), (4, 5, 0, 16, 0)
+)
+RELAYED = (6,)
 
 
 def iota(shape, dim):
@@ -47,7 +50,7 @@
     feats_h, near_h, wanted_h, counts_h, choice_h, conv_h, gain_h, inw_h, outw_h, cot_h,
     layer, grad,
     feats, near_map, wanted, counts, choice, gain, turned,
-    asked, asks, table, answers, own_feats, taps_hot, taps, staged, held,
+    asked, asks, table, answers, own_feats, taps_hot, taps, staged, staged_far, held,
     hidden, qkv, tall, shorts, picked, split_q, scores, cot, att, terms, across, summed, along, final,
     order_taps, order_in, order_out,
     local_sem, send_sem, recv_sem,
@@ -59,6 +62,8 @@
     a = (1 - c) * x + c * y
     b = (1 - c) * y + c * x
     piece = b * 4 + a
+    b_far = lax.rem(b + 2, 4)
+    piece_far = b_far * 4 + a
 
     def z_of(slot):
         return lax.rem(z + NZ - (2 * lax.rem(slot, 2) - 1) * ((slot + 1) // 2), NZ)
@@ -100,21 +105,24 @@
     copies = [
         fetch(cot_h.at[0], cot.at[c], 0),
         fetch(conv_h.at[2 * b, :, lanes], staged.at[0], 1),
+        fetch(conv_h.at[2 * b_far, :, lanes], staged_far.at[0], 12),
         fetch(inw_h.at[pl.ds(0, 8), pl.ds(pl.multiple_of(piece * 128, 128), 128)], staged.at[2], 3),
         fetch(inw_h.at[pl.ds(8, 8), pl.ds(pl.multiple_of(piece * 128, 128), 128)], staged.at[3], 4),
         fetch(outw_h.at[pl.ds(pl.multiple_of(lax.rem(b, 3) * 8, 8), 8), lanes], staged.at[4], 5),
+        fetch(inw_h.at[pl.ds(0, 8), pl.ds(pl.multiple_of(piece_far * 128, 128), 128)], staged_far.at[2], 14),
+        fetch(inw_h.at[pl.ds(8, 8), pl.ds(pl.multiple_of(piece_far * 128, 128), 128)], staged_far.at[3], 15),
     ]
 
-    @pl.when(b < 3)
-    def _():
-        fetch(conv_h.at[2 * b + 1, :, lanes], staged.at[1], 2)
-
-    @pl.when(b == 3)
-    def _():
-        fetch(
-            inw_h.at[pl.ds(pl.multiple_of(lax.rem(a, 2) * 8, 8), 8), pl.ds(pl.multiple_of((16 + a // 2) * 128, 128), 128)],
-            staged.at[1], 2,
-        )
+    for k, (at, to) in enumerate(((b, staged), (b_far, staged_far))):
+
+        @pl.when(at < 3)
+        def _(k=k, at=at, to=to):
+            fetch(conv_h.at[2 * at + 1, :, lanes], to.at[1], 2 + 11 * k)
+
+        @pl.when(at == 3)
+        def _(k=k, to=to):
+            half_rows = pl.ds(pl.multiple_of(lax.rem(a, 2) * 8, 8), 8)
+            fetch(inw_h.at[half_rows, pl.ds(pl.multiple_of((16 + a // 2) * 128, 128), 128)], to.at[1], 2 + 11 * k)
 
     barrier = pltpu.get_barrier_semaphore()
 
@@ -150,7 +158,9 @@
     for copy in copies:
         copy.wait()
     drain(staged.at[1], local_sem.at[2])
+    drain(staged_far.at[1], local_sem.at[13])
     held[piece, :, c, 0] = staged[...]
+    held[piece_far, 0:4, c, 0] = staged_far[...]
     with jax.named_scope("w_barrier"):
         pl.semaphore_wait(barrier, 46)
 
@@ -163,17 +173,18 @@
             send(asks.at[t * 2 + core], asked.at[me], 0, 0, {"z": t, "c": core})
 
     def spread(n):
-        lo, hi, s0, s1 = CHUNKS[n]
+        lo, hi, s0, s1, far = CHUNKS[n]
 
         def one(slot, _):
-            send(staged.at[lo:hi], held.at[piece, lo:hi, c, slot], 5 + n, 7 + n, {"z": z_of(slot)})
+            source, p = (staged_far.at[lo:hi], piece_far) if far else (staged.at[lo:hi], piece)
+            send(source, held.at[p, lo:hi, c, slot], 5 + n, 7 + n, {"z": z_of(slot)})
             return 0
 
         lax.fori_loop(max(s0, 1), s1, one, 0)
 
     far_first(ask)
     send(asks.at[z * 2 + other], asked.at[me], 0, 0, {"c": other})
-    for n in range(4):
+    for n in range(5):
         spread(n)
     send(cot.at[c], cot.at[c], 1, 1, {"c": other})
     for copy in later:
@@ -182,48 +193,53 @@
     order_out[...] = ordering(3, z)
 
     def part(n, p, count, from_slot=None, to_slot=None):
-        lo, hi, s0, s1 = CHUNKS[n]
+        lo, hi, s0, s1, _ = CHUNKS[n]
         return held.at[pl.ds(p, count), lo:hi, c, s0 if from_slot is None else from_slot : s1 if to_slot is None else to_slot]
 
-    def cross(n, p, count, *slots):
-        some = part(n, p, count, *slots)
-        send(some, some, 20 + n, 32 + n, {"c": other})
+    def cross(n, p, count):
+        some = part(n, p, count)
+        send(some, some, 26 + n, 42 + n, {"c": other})
 
     def along_a(n):
-        lo, hi, s0, s1 = CHUNKS[n]
+        lo, hi, s0, s1, far = CHUNKS[n]
         with jax.named_scope(f"w_z{n}"):
             drain(held.at[0, lo:hi, 0, max(s0, 1) : s1], recv_sem.at[7 + n])
+        some = part(n, piece_far if far else piece, 1)
         for d in (2, 1, 3):
-            send(part(n, piece, 1), part(n, piece, 1), 10 + n, 12 + n, a_peer(d)[1])
+            send(some, some, 12 + n, 14 + n, a_peer(d)[1])
 
     def along_b(n):
-        lo, hi, s0, s1 = CHUNKS[n]
+        lo, hi, s0, s1, far = CHUNKS[n]
         with jax.named_scope(f"w_a{n}"):
-            drain(held.at[0:3, lo:hi, 0, s0:s1], recv_sem.at[12 + n])
-        for k, d in enumerate((1, 3)):
-            send(part(n, b * 4, 4), part(n, b * 4, 4), 15 + n, 17 + 5 * k + n, b_peer(d)[1])
-        cross(n, b * 4, 4)
+            drain(held.at[0:3, lo:hi, 0, s0:s1], recv_sem.at[14 + n])
+        if not far:
+            for k, d in enumerate((1, 3)):
+                send(part(n, b * 4, 4), part(n, b * 4, 4), 19 + n, 21 + 7 * k + n, b_peer(d)[1])
+        cross(n, (b_far if far else b) * 4, 4)
 
     def relay(n):
-        lo, hi, s0, s1 = CHUNKS[n]
+        lo, hi, s0, s1, _ = CHUNKS[n]
         middle = (s0 + s1) // 2
         for k, d, low, high in ((0, 1, s0, middle), (1, 3, middle, s1)):
             source = lax.rem(b + 4 - d, 4) * 4
             with jax.named_scope(f"w_b{n}"):
-                drain(part(n, source, 4), recv_sem.at[17 + 5 * k + n])
-            send(part(n, source, 4, low, high), part(n, source, 4, low, high), 15 + n, 27 + n, b_peer(d)[1])
+                drain(part(n, source, 4), recv_sem.at[21 + 7 * k + n])
+            if n in RELAYED:
+                send(part(n, source, 4, low, high), part(n, source, 4, low, high), 19 + n, 35 + n, b_peer(d)[1])
             cross(n, source, 4)
 
     def last(n):
-        source = lax.rem(b + 2, 4) * 4
         with jax.named_scope(f"w_f{n}"):
-            drain(part(n, source, 4), recv_sem.at[27 + n])
-        cross(n, source, 4)
+            drain(part(n, b_far * 4, 4), recv_sem.at[35 + n])
+        cross(n, b_far * 4, 4)
+
+    def crossings(n):
+        return 16 if n in RELAYED else 4 if CHUNKS[n][4] else 12
 
     def crossed(n):
-        lo, hi, s0, s1 = CHUNKS[n]
+        lo, hi, s0, s1, _ = CHUNKS[n]
         with jax.named_scope(f"w_c{n}"):
-            drain(held.at[:, lo:hi, 0, s0:s1], recv_sem.at[32 + n])
+            drain(held.at[0 : crossings(n), lo:hi, 0, s0:s1], recv_sem.at[42 + n])
 
     along_a(0)
 
@@ -244,20 +260,19 @@
 
     far_first(answer)
     send(answers.at[z * 2 + other], table.at[16 + me], 2, 2, {"c": other})
-    spread(4)
+    spread(5)
+    spread(6)
 
     along_b(0)
     along_a(1)
     along_a(2)
+    along_a(3)
+    along_b(1)
     relay(0)
-    along_b(1)
-    along_a(3)
+    along_a(4)
     along_b(2)
+    along_b(3)
     relay(1)
-    last(0)
-    along_b(3)
-    relay(2)
-    last(1)
     with jax.named_scope("w_rows"):
         drain(table.at[0:31], recv_sem.at[2])
     fetched = table[16:48].reshape(256, 256)
@@ -265,10 +280,9 @@
     for k in range(3):
         got = dot(taps_hot[256 * k : 256 * (k + 1), :], table[...].reshape(384, 256))
         taps[2 * k : 2 * k + 2] = got.astype(BF16).reshape(2, 128, 256)
-    relay(3)
-    last(2)
-    crossed(0)
-    crossed(1)
+    for n in range(4):
+        crossed(n)
+    along_b(4)
 
     def unit(p, u):
         return held[p, u].reshape(256, 128)
@@ -286,12 +300,31 @@
     h = hidden[...]
     power = jnp.mean(h * h, axis=-1, keepdims=True)
     normed = (h * lax.rsqrt(power + 1e-06) * gain[...]).astype(BF16)
+
+    token = iota((8, 128), 1)
+    block_mask = one_hot(((token >> 6) == iota((8, 128), 0)) & (token < count))
+    number = jnp.clip(count - 64 * iota((8, 1), 0), 0, 64)
+    means = dot(block_mask, normed) / jnp.maximum(number, 1).astype(F32)
+    for j in range(4):
+        tall[2 * j : 2 * j + 2, :] = means[0:2, 128 * j : 128 * (j + 1)]
+    shorts[me] = tall[...].astype(BF16)
+
+    def tell(slot):
+        for core in range(2):
+            send(shorts.at[me], shorts.at[me], 3, 3, {"z": z_of(slot), "c": core})
+
+    far_first(tell)
+    send(shorts.at[me], shorts.at[me], 3, 3, {"c": other})
+
     normed = dot(normed, order_in[...]).astype(BF16)
-    last(3)
-    crossed(2)
-    crossed(3)
-
-    def project(j):
+    along_a(5)
+    relay(4)
+    along_b(5)
+    along_a(6)
+    crossed(4)
+    crossed(5)
+
+    def project(rows, j):
         upper, lower = [], []
         for t in (j, j + 1):
             if t < 16:
@@ -300,27 +333,12 @@
             else:
                 upper.append(unit(12 + 2 * (t - 16), 1))
                 lower.append(unit(13 + 2 * (t - 16), 1))
-        got = dot(normed[:, :256], jnp.concatenate(upper, axis=1))
-        got = got + dot(normed[:, 256:], jnp.concatenate(lower, axis=1))
-        qkv[:, 128 * j : 128 * (j + 2)] = got.astype(BF16)
-
-    for j in range(6, 18, 2):
-        project(j)
-
-    token = iota((8, 128), 1)
-    block_mask = one_hot(((token >> 6) == iota((8, 128), 0)) & (token < count))
-    sums = dot(block_mask, qkv[:, 768:])
-    number = jnp.clip(count - 64 * iota((8, 1), 0), 0, 64)
-    means = sums / jnp.maximum(number, 1).astype(F32)
-    for j in range(12):
-        tall[2 * j : 2 * j + 2, :] = means[0:2, 128 * j : 128 * (j + 1)]
-    shorts[c, z] = tall[...].astype(BF16).reshape(3, 8, 128)
-
-    far_first(lambda slot: send(shorts.at[c, z], shorts.at[c, z], 3, 3, {"z": z_of(slot)}))
-    along_a(4)
-
-    for j in range(0, 6, 2):
-        project(j)
+        got = dot(rows[:, :256], jnp.concatenate(upper, axis=1))
+        return (got + dot(rows[:, 256:], jnp.concatenate(lower, axis=1))).astype(BF16)
+
+    for j in range(0, 18, 2):
+        qkv[:, 128 * j : 128 * (j + 2)] = project(normed, j)
+
     half = iota((128, 128), 1) < 64
     row256 = iota((256, 128), 0) & 127
     col256 = iota((256, 128), 1)
@@ -331,41 +349,37 @@
         q = jnp.concatenate([jnp.where(half, q, none), jnp.where(half, none, q)], axis=0)
         split_q[j] = q
         scores[j] = jnp.where(near_ok, dot_t(q, qkv[:, 768 + 128 * j : 768 + 128 * (j + 1)]), -1e30)
-    m96 = iota((96, 1), 0)
-    target = jnp.zeros((96, 1), jnp.int32)
+    m32 = iota((32, 1), 0)
+    target = jnp.zeros((32, 1), jnp.int32)
     for e in range(8):
         block = choice[0, e // 4, e % 4]
-        shard = block // 2
-        start = (lax.rem(shard, 2) * 16 + shard // 2) * 24 + lax.rem(block, 2)
-        target = jnp.where((m96 & 7) == e, start, target)
-    target = target + 2 * (m96 >> 3)
-    chosen_hot = one_hot(target == iota((96, 768), 1))
-    along_b(4)
-    relay(4)
-    last(4)
-
+        target = jnp.where((m32 & 7) == e, (block // 2) * 8 + lax.rem(block, 2), target)
+    chosen_hot = one_hot(target + 2 * (m32 >> 3) == iota((32, 256), 1))
+
+    along_b(6)
     with jax.named_scope("w_short"):
-        drain(shorts.at[0, 0:15], recv_sem.at[3])
-    send(shorts.at[c], shorts.at[c], 4, 4, {"c": other})
-    with jax.named_scope("w_shortc"):
-        drain(shorts.at[0], recv_sem.at[4])
-    picked[...] = dot(chosen_hot, shorts[...].reshape(768, 128))
+        drain(shorts.at[0:31], recv_sem.at[3])
+    chosen = dot(chosen_hot, shorts[...].reshape(256, 128))
+    chosen = jnp.concatenate([chosen[8 * j : 8 * j + 8] for j in range(4)], axis=1).astype(BF16)
+    chosen = dot(chosen, order_in[...]).astype(BF16)
+    for j in range(6, 18, 2):
+        picked[:, 128 * (j - 6) : 128 * (j - 4)] = project(chosen, j)
     far_ok = ((iota((256, 8), 0) & 127) >> 6) == (iota((256, 8), 1) >> 2)
     for j in range(6):
         near = scores[j]
-        far = dot_t(split_q[j], picked[8 * j : 8 * j + 8, :].astype(BF16))
+        far = dot_t(split_q[j], picked[:, 128 * j : 128 * (j + 1)])
         far = jnp.where(far_ok, far, -1e30)
         top = jnp.maximum(jnp.max(near, axis=1, keepdims=True), jnp.max(far, axis=1, keepdims=True))
         near, far = jnp.exp(near - top), jnp.exp(far - top)
         scale = 1.0 / (jnp.sum(near, axis=1, keepdims=True) + jnp.sum(far, axis=1, keepdims=True))
         near, far = (near * scale).astype(BF16), (far * scale).astype(BF16)
         mixed = dot(near, qkv[:, 1536 + 128 * j : 1536 + 128 * (j + 1)])
-        mixed = mixed + dot(far, picked[48 + 8 * j : 56 + 8 * j, :].astype(BF16))
+        mixed = mixed + dot(far, picked[:, 768 + 128 * j : 768 + 128 * (j + 1)])
         mixed = jnp.where(half, mixed[:128], mixed[128:]) * alive
         att[c, :, 128 * j : 128 * (j + 1)] = mixed.astype(BF16)
         if j % 3 == 2:
             part_of = att.at[c, :, 128 * (j - 2) : 128 * (j + 1)]
-            send(part_of, part_of, 25 + j // 3, 5 + j // 3, {"c": other})
+            send(part_of, part_of, 33 + j // 3, 5 + j // 3, {"c": other})
 
     drain(cot.at[0], recv_sem.at[1])
     for g in range(2):
@@ -382,9 +396,30 @@
                 terms[t + k, rows] = got[:, 128 * k : 128 * (k + 1)].astype(BF16).reshape(8, 2, 3, 8, 128)
         for d in (2, 1, 3):
             t, where = a_peer(d)
-            send(terms.at[t, rows, c], across.at[d - 1, rows], 27 + g, 37 + g, where)
-
-    crossed(4)
+            send(terms.at[t, rows, c], across.at[d - 1, rows], 35 + g, 49 + g, where)
+
+    relay(6)
+    for g in range(2):
+        rows = slice(8 * g, 8 * (g + 1))
+        with jax.named_scope(f"w_across{g}"):
+            drain(across.at[:, rows], recv_sem.at[49 + g])
+        total = terms[a, rows, c].astype(F32)
+        for d in range(3):
+            total = total + across[d, rows].astype(F32)
+        summed[rows] = total.astype(BF16)
+
+        def reduce_z(t, _):
+            @pl.when(t != z)
+            def _():
+                send(summed.at[t], along.at[z], 37, 51, {"z": t})
+
+            return 0
+
+        lax.fori_loop(8 * g, 8 * (g + 1), reduce_z, 0)
+    along[z] = summed[z]
+
+    last(6)
+    crossed(6)
     attended = dot(att[c], order_out[...]).astype(BF16)
     for t in range(0, 4, 2):
         total = hidden[:, 128 * t : 128 * (t + 2)]
@@ -393,38 +428,20 @@
             total = total + dot(attended[:, 256 * i : 256 * (i + 1)], w)
         layer[0, :, 128 * t : 128 * (t + 2)] = total.astype(BF16)
 
-    for g in range(2):
-        rows = slice(8 * g, 8 * (g + 1))
-        with jax.named_scope(f"w_across{g}"):
-            drain(across.at[:, rows], recv_sem.at[37 + g])
-        total = terms[a, rows, c].astype(F32)
-        for d in range(3):
-            total = total + across[d, rows].astype(F32)
-        summed[rows] = total.astype(BF16)
-
-        def reduce_z(t, _):
-            @pl.when(t != z)
-            def _():
-                send(summed.at[t], along.at[z], 29, 39, {"z": t})
-
-            return 0
-
-        lax.fori_loop(8 * g, 8 * (g + 1), reduce_z, 0)
-    along[z] = summed[z]
     with jax.named_scope("w_along"):
-        drain(along.at[0:15], recv_sem.at[39])
+        drain(along.at[0:15], recv_sem.at[51])
     total = along[0].astype(F32)
     for k in range(1, NZ):
         total = total + along[k].astype(F32)
     final[piece] = total.astype(BF16)
 
     def show(k, _):
-        send(final.at[piece], final.at[piece], 30, 40, plane_peer(k))
+        send(final.at[piece], final.at[piece], 38, 52, plane_peer(k))
         return 0
 
     lax.fori_loop(1, 16, show, 0)
     with jax.named_scope("w_final"):
-        drain(final.at[0:15], recv_sem.at[40])
+        drain(final.at[0:15], recv_sem.at[52])
     factor = (16 * 4096) ** -0.5
     for t in range(4):
         total = final[t].astype(F32)
@@ -435,18 +452,18 @@
     drain(asked.at[0:31], send_sem.at[0])
     drain(cot.at[0], send_sem.at[1])
     drain(table.at[0:31], send_sem.at[2])
-    drain(shorts.at[0, 0:15], send_sem.at[3])
-    drain(shorts.at[0], send_sem.at[4])
-    for n, (lo, hi, s0, s1) in enumerate(CHUNKS):
+    drain(shorts.at[0:31], send_sem.at[3])
+    for n, (lo, hi, s0, s1, far) in enumerate(CHUNKS):
         drain(held.at[0, lo:hi, 0, max(s0, 1) : s1], send_sem.at[5 + n])
-        drain(held.at[0:3, lo:hi, 0, s0:s1], send_sem.at[10 + n])
-        drain(held.at[0:12, lo:hi, 0, s0:s1], send_sem.at[15 + n])
-        drain(held.at[:, lo:hi, 0, s0:s1], send_sem.at[20 + n])
+        drain(held.at[0:3, lo:hi, 0, s0:s1], send_sem.at[12 + n])
+        if not far:
+            drain(held.at[0 : 12 if n in RELAYED else 8, lo:hi, 0, s0:s1], send_sem.at[19 + n])
+        drain(held.at[0 : crossings(n), lo:hi, 0, s0:s1], send_sem.at[26 + n])
     for g in range(2):
-        drain(att.at[0, :, 384 * g : 384 * (g + 1)], send_sem.at[25 + g])
-        drain(across.at[:, 8 * g : 8 * (g + 1)], send_sem.at[27 + g])
-    drain(along.at[0:15], send_sem.at[29])
-    drain(final.at[0:15], send_sem.at[30])
+        drain(att.at[0, :, 384 * g : 384 * (g + 1)], send_sem.at[33 + g])
+        drain(across.at[:, 8 * g : 8 * (g + 1)], send_sem.at[35 + g])
+    drain(along.at[0:15], send_sem.at[37])
+    drain(final.at[0:15], send_sem.at[38])
 
 
 def shards(feats, near_map, wanted, counts, choice, conv, gain, inw, outw, cot):
@@ -475,12 +492,13 @@
             v((768, 384), BF16),
             v((6, 128, 256), BF16),
             v((5, 8, 128), BF16),
+            v((4, 8, 128), BF16),
             v((16, 5, 2, NZ, 8, 128), BF16),
             v((128, 512), F32),
             v((128, 2304), BF16),
-            v((24, 128), F32),
-            v((2, NZ, 3, 8, 128), BF16),
-            v((96, 128), F32),
+            v((8, 128), F32),
+            v((32, 8, 128), BF16),
+            v((8, 1536), BF16),
             v((6, 256, 128), BF16),
             v((6, 256, 128), F32),
             v((2, 128, 512), BF16),
@@ -493,9 +511,9 @@
             v((256, 256), BF16),
             v((512, 512), BF16),
             v((768, 768), BF16),
-            pltpu.SemaphoreType.DMA((12,)),
-            pltpu.SemaphoreType.DMA((31,)),
-            pltpu.SemaphoreType.DMA((41,)),
+            pltpu.SemaphoreType.DMA((16,)),
+            pltpu.SemaphoreType.DMA((39,)),
+            pltpu.SemaphoreType.DMA((53,)),
         ],
         compiler_params=pltpu.CompilerParams(
             collective_id=0, has_side_effects=True, vmem_limit_bytes=VMEM

time: 80.2 us -> 71.6 us (0.89)
  Pallas kernels: 77.5 us -> 69.1 us
    pallas_call x1, Pallas kernels: 77.5 us -> 69.1 us  [shards(): pl.pallas_call(kernel, name='layer', out_shape=(jax.ShapeDtypeStruct((1,...]
where the time goes in v3:
time: 71.6 us; the launch traced here: 71 us
  Pallas kernels  69.1 us (97%)
  local copies, waits for them, and re-layouts  1.28 us (2%)
    pallas_call x1, Pallas kernels, shards(): pl.pallas_call(kernel, name='layer', out_shape=(jax.ShapeDtypeStruct((1,...  69.1 us

profile of v3, /device:TPU:1, one launch (start us, length us, event | category | flops | bytes accessed | tf_op | source)
XLA Modules:
  0.0 71.0 jit_solution(5259066546013146944)
XLA Ops:
  0.6 69.1 %layer.1 = (bf16[1,128,512]{2,1,0:T(8,128)(2,1)S(1)}, f32[24,512]{1,0:T(8,128)S(1)}) custom-call(bf16[1,128,256]{2,1,0:T(8,128)(2,1)} %feats_h.1, s32[6,1,128]{2,1,0:T(1,128)} %bitcast.4, s32[1,1,8,32]{3,2,1,0:T(8,128)} %bitcast.3, s32[1,32]{1,0:T(1,128)} %counts_h.1, s32[1,2,4]{2,1,0:T(2,128)} %choice_h.1, bf16[7,8,512]{2,1,0:T(8,128)(2,1)} %conv_h.1, ...), custom_call_target="tpu_custom_call" | custom-call | tf_op jit(solution)/shard_map/layer/pallas_call | solution.py:473
  69.7 0.7 copy.14
  70.4 0.6 copy.15

commit v4 on v3

v4 whole, which is shorter than its diff:
```python
import jax
import jax.numpy as jnp
from jax import lax
from jax.experimental import pallas as pl
from jax.experimental.pallas import tpu as pltpu
from jax.sharding import Mesh
from jax.sharding import PartitionSpec as P

MESH = pl.DeviceIdType.MESH
F32 = jnp.float32
BF16 = jnp.bfloat16
NZ = 16
VMEM = 48 * 1024 * 1024
CHUNKS = {0: (0, 2, 0, 8, 0), 1: (0, 2, 8, 16, 0), 2: (0, 2, 0, 8, 1), 3: (0, 2, 8, 16, 1), 7: (2, 3, 0, 16, 0)}
RELAYED = (7,)
SPLIT = {4: (0, 8, 0), 5: (8, 16, 0), 6: (0, 16, 1)}


def iota(shape, dim):
    return lax.broadcasted_iota(jnp.int32, shape, dim)


def one_hot(flags):
    return jnp.where(flags, 1.0, 0.0).astype(BF16)


def ordering(parts, z):
    n = 256 * parts
    col = iota((1, n), 1)
    slot = (col >> 3) & 15
    chip = (z + NZ + jnp.where((slot & 1) == 1, (slot + 1) >> 1, -(slot >> 1))) & 15
    natural = chip * (16 * parts) + ((col >> 7) & 1) * (8 * parts) + (col >> 8) * 8 + (col & 7)
    return one_hot(iota((n, n), 0) == natural)


def dot(a, b):
    return jnp.dot(a, b, preferred_element_type=F32)


def dot_t(a, b):
    return lax.dot_general(a, b, (((1,), (1,)), ((), ())), preferred_element_type=F32)


def turned_dot(a, b):
    return lax.dot_general(a, b, (((0,), (0,)), ((), ())), preferred_element_type=F32)


def drain(ref, sem):
    pltpu.make_async_copy(ref, ref, sem).wait()


def kernel(
    feats_h, near_h, wanted_h, counts_h, choice_h, conv_h, gain_h, inw_h, outw_h, cot_h,
    layer, grad,
    feats, near_map, wanted, counts, choice, gain, turned,
    asked, asks, table, answers, own_feats, taps_hot, taps, staged, staged_far, staged_in, held, split_in,
    hidden, normed_all, qkv, tall, shorts, chosen_hot, picked, split_q, near_mix, near_top, near_sum, cot, att, att_all, terms, across, summed, along, final,
    order_taps, order_in, order_out,
    local_sem, send_sem, recv_sem,
):
    y, x, z, c = (lax.axis_index(n) for n in ("y", "x", "z", "c"))
    other = 1 - c
    me = z * 2 + c
    plane = y * 4 + x
    a = (1 - c) * x + c * y
    b = (1 - c) * y + c * x
    piece = b * 4 + a
    b_far = lax.rem(b + 2, 4)
    piece_far = b_far * 4 + a
    core_pieces = ((y * 4 + x, lax.rem(y + 2, 4) * 4 + x), (x * 4 + y, lax.rem(x + 2, 4) * 4 + y))

    def z_of(slot):
        return lax.rem(z + NZ - (2 * lax.rem(slot, 2) - 1) * ((slot + 1) // 2), NZ)

    def a_peer(d):
        t = lax.rem(a + d, 4)
        return t, {"x": (1 - c) * t + c * x, "y": (1 - c) * y + c * t}

    def b_peer(d):
        t = lax.rem(b + d, 4)
        return t, {"x": (1 - c) * x + c * t, "y": (1 - c) * t + c * y}

    def plane_peer(k):
        t = lax.rem(plane + k, 16)
        return {"y": t // 4, "x": lax.rem(t, 4)}

    def send(src, dst, s, r, where):
        pltpu.make_async_remote_copy(
            src_ref=src, dst_ref=dst, send_sem=send_sem.at[s], recv_sem=recv_sem.at[r],
            device_id=where, device_id_type=MESH,
        ).start()

    def fetch(src, dst, k):
        copy = pltpu.make_async_copy(src, dst, local_sem.at[k])
        copy.start()
        return copy

    first = [
        fetch(wanted_h, wanted, 6),
        fetch(near_h, near_map, 7),
        fetch(feats_h.at[0], feats, 8),
    ]

    barrier = pltpu.get_barrier_semaphore()

    def hail(where):
        pl.semaphore_signal(barrier, inc=1, device_id=where, device_id_type=MESH)

    def hail_z(i, _):
        hail({"z": z_of(i), "c": 0})
        hail({"z": z_of(i), "c": 1})
        return 0

    lax.fori_loop(1, NZ, lambda i, _: hail_z(NZ - i, _), 0)
    lax.fori_loop(1, 16, lambda k, _: (hail(plane_peer(k)), 0)[1], 0)
    hail({"c": other})

    lanes = pl.ds(pl.multiple_of(a * 128, 128), 128)
    later = [
        fetch(counts_h, counts, 9),
        fetch(choice_h, choice, 10),
        fetch(gain_h, gain, 11),
    ]
    copies = [
        fetch(cot_h.at[0], cot.at[c], 0),
        fetch(conv_h.at[2 * b, :, lanes], staged.at[0], 1),
        fetch(conv_h.at[2 * b_far, :, lanes], staged_far.at[0], 12),
        fetch(outw_h.at[pl.ds(pl.multiple_of(lax.rem(b, 3) * 8, 8), 8), lanes], staged.at[2], 5),
        *(
            fetch(
                inw_h.at[
                    pl.ds(pl.multiple_of(lax.rem(p, 2) * 8, 8), 8),
                    pl.ds(pl.multiple_of((p // 6 * 6 + 3 * h + lax.rem(p // 2, 3)) * 128, 128), 128),
                ],
                staged_in.at[h, far], 16 + 2 * h + far,
            )
            for h in range(2) for far, p in enumerate(core_pieces[h])
        ),
    ]

    for k, (at, to) in enumerate(((b, staged), (b_far, staged_far))):

        @pl.when(at < 3)
        def _(k=k, at=at, to=to):
            fetch(conv_h.at[2 * at + 1, :, lanes], to.at[1], 2 + 11 * k)

        @pl.when(at == 3)
        def _(k=k, to=to):
            half_rows = pl.ds(pl.multiple_of(lax.rem(a, 2) * 8, 8), 8)
            fetch(inw_h.at[half_rows, pl.ds(pl.multiple_of((14 + 3 * (a // 2)) * 128, 128), 128)], to.at[1], 2 + 11 * k)

    turned[...] = jnp.zeros_like(turned)
    for copy in first:
        copy.wait()
    turned[0, 0:8, 0:32] = wanted[0, 0].astype(F32)
    for k in range(6):
        turned[1, k : k + 1, :] = near_map[k].astype(F32)
    lists = turned[0].T[0:32].astype(jnp.int32)
    slots = jnp.zeros((32, 128), jnp.int32)
    for k in range(8):
        slots = slots + jnp.where(lists[:, k : k + 1] == iota((32, 128), 1), 1 << k, 0)
    for p in range(32):
        asks[p] = slots[p : p + 1, :]
    asked[me] = asks[me]
    rows = turned[1].T
    for k in range(6):
        taps_hot[128 * k : 128 * (k + 1), :] = one_hot(rows[:, k : k + 1].astype(jnp.int32) == iota((128, 384), 1))
    order_taps[...] = ordering(1, z)
    ordered = dot(feats[...], order_taps[...]).astype(BF16)
    own_feats[...] = ordered
    table[0:16] = ordered.reshape(16, 8, 256)
    for copy in copies:
        copy.wait()
    drain(staged.at[1], local_sem.at[2])
    drain(staged_far.at[1], local_sem.at[13])
    held[piece, :, c, 0] = staged[...]
    held[piece_far, 0:2, c, 0] = staged_far[...]
    split_in[piece, c, 0] = staged_in[c, 0]
    split_in[piece_far, c, 0] = staged_in[c, 1]
    with jax.named_scope("w_barrier"):
        pl.semaphore_wait(barrier, 46)

    def far_first(body):
        lax.fori_loop(1, NZ, lambda i, _: (body(NZ - i), 0)[1], 0)

    def ask(slot):
        t = z_of(slot)
        for core in range(2):
            send(asks.at[t * 2 + core], asked.at[me], 0, 0, {"z": t, "c": core})

    def spread(n):
        lo, hi, s0, s1, far = CHUNKS[n]

        def one(slot, _):
            source, p = (staged_far.at[lo:hi], piece_far) if far else (staged.at[lo:hi], piece)
            send(source, held.at[p, lo:hi, c, slot], 5 + n, 7 + n, {"z": z_of(slot)})
            return 0

        lax.fori_loop(max(s0, 1), s1, one, 0)

    def spread_in(n):
        s0, s1, far = SPLIT[n]

        def one(slot, _):
            for h in range(2):
                send(staged_in.at[h, far], split_in.at[core_pieces[h][far], c, slot], 5 + n, 7 + n, {"z": z_of(slot), "c": h})
            return 0

        if s0 == 0:
            p = (1 - other) * core_pieces[0][far] + other * core_pieces[1][far]
            send(staged_in.at[other, far], split_in.at[p, c, 0], 5 + n, 7 + n, {"c": other})
        lax.fori_loop(max(s0, 1), s1, one, 0)

    def arrivals(n):
        return (split_in.at[0, 0, 0:15], split_in.at[0, 0], shorts.at[0:31])[n - 4]

    far_first(ask)
    send(asks.at[z * 2 + other], asked.at[me], 0, 0, {"c": other})
    for n in range(4):
        spread(n)
    spread_in(4)
    spread_in(5)
    send(cot.at[c], cot.at[c], 1, 1, {"c": other})
    for copy in later:
        copy.wait()
    m32 = iota((32, 1), 0)
    target = jnp.zeros((32, 1), jnp.int32)
    for e in range(8):
        block = choice[0, e // 4, e % 4]
        target = jnp.where((m32 & 7) == e, (block // 2) * 8 + lax.rem(block, 2), target)
    chosen_hot[c] = one_hot(target + 2 * (m32 >> 3) == iota((32, 256), 1))
    order_in[...] = ordering(2, z)
    order_out[...] = ordering(3, z)

    def part(n, p, count, from_slot=None, to_slot=None):
        lo, hi, s0, s1, _ = CHUNKS[n]
        return held.at[pl.ds(p, count), lo:hi, c, s0 if from_slot is None else from_slot : s1 if to_slot is None else to_slot]

    def cross(n, p, count):
        some = part(n, p, count)
        send(some, some, 29 + n, 47 + n, {"c": other})

    def along_a(n):
        lo, hi, s0, s1, far = CHUNKS[n]
        with jax.named_scope(f"w_z{n}"):
            drain(held.at[0, lo:hi, 0, max(s0, 1) : s1], recv_sem.at[7 + n])
        some = part(n, piece_far if far else piece, 1)
        for d in (2, 1, 3):
            send(some, some, 13 + n, 15 + n, a_peer(d)[1])

    def along_b(n):
        lo, hi, s0, s1, far = CHUNKS[n]
        with jax.named_scope(f"w_a{n}"):
            drain(held.at[0:3, lo:hi, 0, s0:s1], recv_sem.at[15 + n])
        if not far:
            for k, d in enumerate((1, 3)):
                send(part(n, b * 4, 4), part(n, b * 4, 4), 21 + n, 23 + 8 * k + n, b_peer(d)[1])
        cross(n, (b_far if far else b) * 4, 4)

    def relay(n):
        lo, hi, s0, s1, _ = CHUNKS[n]
        middle = (s0 + s1) // 2
        for k, d, low, high in ((0, 1, s0, middle), (1, 3, middle, s1)):
            source = lax.rem(b + 4 - d, 4) * 4
            with jax.named_scope(f"w_b{n}"):
                drain(part(n, source, 4), recv_sem.at[23 + 8 * k + n])
            if n in RELAYED:
                send(part(n, source, 4, low, high), part(n, source, 4, low, high), 21 + n, 39 + n, b_peer(d)[1])
            cross(n, source, 4)

    def last(n):
        with jax.named_scope(f"w_f{n}"):
            drain(part(n, b_far * 4, 4), recv_sem.at[39 + n])
        cross(n, b_far * 4, 4)

    def part_in(n, p, count):
        s0, s1, _ = SPLIT[n]
        return split_in.at[pl.ds(p, count), :, s0:s1]

    def split_a(n):
        with jax.named_scope(f"w_z{n}"):
            drain(arrivals(n), recv_sem.at[7 + n])
        some = part_in(n, piece_far if SPLIT[n][2] else piece, 1)
        for d in (2, 1, 3):
            send(some, some, 13 + n, 15 + n, a_peer(d)[1])

    def split_b(n):
        with jax.named_scope(f"w_a{n}"):
            drain(part_in(n, 0, 3), recv_sem.at[15 + n])
        if not SPLIT[n][2]:
            for k, d in enumerate((1, 3)):
                send(part_in(n, b * 4, 4), part_in(n, b * 4, 4), 21 + n, 23 + 8 * k + n, b_peer(d)[1])

    def split_end(n):
        for k, d in ((0, 1), (1, 3)):
            with jax.named_scope(f"w_b{n}"):
                drain(part_in(n, lax.rem(b + 4 - d, 4) * 4, 4), recv_sem.at[23 + 8 * k + n])

    def crossings(n):
        return 16 if n in RELAYED else 4 if CHUNKS[n][4] else 12

    def crossed(n):
        lo, hi, s0, s1, _ = CHUNKS[n]
        with jax.named_scope(f"w_c{n}"):
            drain(held.at[0 : crossings(n), lo:hi, 0, s0:s1], recv_sem.at[47 + n])

    send(chosen_hot.at[c], chosen_hot.at[c], 4, 4, {"c": other})
    along_a(0)

    with jax.named_scope("w_ask"):
        drain(asked.at[0:31], recv_sem.at[0])
    wants = jnp.broadcast_to(asked[...], (32, 8, 128))
    wants = one_hot(((wants >> iota((32, 8, 128), 1)) & 1) == 1).reshape(256, 128)
    picked_rows = dot(wants, feats[...]).astype(BF16)
    answers[...] = picked_rows.reshape(32, 8, 256)
    table[16 + me] = answers[me]

    def answer(slot):
        t = z_of(slot)
        for core in range(2):
            send(answers.at[t * 2 + core], table.at[16 + me], 2, 2, {"z": t, "c": core})

    far_first(answer)
    send(answers.at[z * 2 + other], table.at[16 + me], 2, 2, {"c": other})
    spread_in(6)
    spread(7)

    along_a(1)
    along_b(0)
    along_a(2)
    along_a(3)
    along_b(1)
    relay(0)
    split_a(4)
    split_a(5)
    along_b(2)
    along_b(3)
    relay(1)
    with jax.named_scope("w_rows"):
        drain(table.at[0:31], recv_sem.at[2])
    fetched = table[16:48].reshape(256, 256)
    table[16:48] = dot(fetched, order_taps[...]).astype(BF16).reshape(32, 8, 256)
    for k in range(3):
        got = dot(taps_hot[256 * k : 256 * (k + 1), :], table[...].reshape(384, 256))
        taps[2 * k : 2 * k + 2] = got.astype(BF16).reshape(2, 128, 256)
    split_b(4)
    for n in range(4):
        crossed(n)
    split_b(5)

    def unit(p, u):
        return held[p, u].reshape(256, 128)

    count = counts[0, me]
    alive = jnp.where(iota((128, 128), 0) < count, 1.0, 0.0)
    alive_wide = jnp.concatenate([alive, alive], axis=1)
    for t in range(0, 4, 2):
        total = jnp.zeros((128, 256), F32)
        for k in range(7):
            p, u = (k // 2) * 4 + t, k % 2
            tap = own_feats[...] if k == 0 else taps[k - 1]
            total = total + dot(tap, jnp.concatenate([unit(p, u), unit(p + 1, u)], axis=1))
        hidden[:, 128 * t : 128 * (t + 2)] = total * alive_wide
    h = hidden[...]
    power = jnp.mean(h * h, axis=-1, keepdims=True)
    normed = (h * lax.rsqrt(power + 1e-06) * gain[...]).astype(BF16)

    token = iota((8, 128), 1)
    block_mask = one_hot(((token >> 6) == iota((8, 128), 0)) & (token < count))
    number = jnp.clip(count - 64 * iota((8, 1), 0), 0, 64)
    means = dot(block_mask, normed) / jnp.maximum(number, 1).astype(F32)
    for j in range(4):
        tall[2 * j : 2 * j + 2, :] = means[0:2, 128 * j : 128 * (j + 1)]
    shorts[me] = tall[...].astype(BF16)

    def tell(slot):
        for core in range(2):
            send(shorts.at[me], shorts.at[me], 3, 3, {"z": z_of(slot), "c": core})

    far_first(tell)
    send(shorts.at[me], shorts.at[me], 3, 3, {"c": other})

    normed_all[c] = dot(normed, order_in[...]).astype(BF16)
    send(normed_all.at[c], normed_all.at[c], 38, 6, {"c": other})
    split_a(6)
    split_end(4)
    along_a(7)
    with jax.named_scope("w_norm"):
        drain(normed_all.at[0], recv_sem.at[6])
    split_end(5)
    split_b(6)

    def unit_in(tile, i):
        if tile < 8:
            return split_in[2 * tile + i].reshape(256, 128)
        return held[12 + 2 * c + i, 1].reshape(256, 128)

    def project(rows, tiles):
        upper = jnp.concatenate([unit_in(t, 0) for t in tiles], axis=1)
        lower = jnp.concatenate([unit_in(t, 1) for t in tiles], axis=1)
        return dot(rows[:, :256], upper) + dot(rows[:, 256:], lower)

    tokens = normed_all[...].reshape(256, 512)
    for tiles in ((0, 1), (2, 3), (4, 5), (6, 7), (8,)):
        qkv[:, 128 * tiles[0] : 128 * (tiles[-1] + 1)] = project(tokens, tiles).astype(BF16)

    half = iota((128, 128), 1) < 64
    key = iota((128, 256), 0)
    same_block = (key >> 6) == ((iota((128, 256), 1) & 127) >> 6)
    for core in range(2):
        near_ok = same_block & (key < counts[0, 2 * z + core])
        rows = slice(128 * core, 128 * (core + 1))
        for j in range(3):
            at = 3 * core + j
            q = qkv[rows, 128 * j : 128 * (j + 1)] * jnp.asarray(0.125, BF16)
            none = jnp.zeros_like(q)
            q = jnp.concatenate([jnp.where(half, q, none), jnp.where(half, none, q)], axis=0)
            split_q[at] = q
            near = jnp.where(near_ok, dot_t(qkv[rows, 384 + 128 * j : 384 + 128 * (j + 1)], q), -1e30)
            top = jnp.max(near, axis=0, keepdims=True)
            near = jnp.exp(near - top)
            near_top[at] = top
            near_sum[at] = jnp.sum(near, axis=0, keepdims=True)
            mixed = turned_dot(qkv[rows, 768 + 128 * j : 768 + 128 * (j + 1)], near.astype(BF16))
            near_mix[at, 0:64] = mixed[0:64, 0:128]
            near_mix[at, 64:128] = mixed[64:128, 128:256]
    drain(chosen_hot.at[0], recv_sem.at[4])
    drain(cot.at[0], recv_sem.at[1])

    with jax.named_scope("w_short"):
        drain(shorts.at[0:31], recv_sem.at[3])
    chosen = dot(chosen_hot[...].reshape(64, 256), shorts[...].reshape(256, 128))
    chosen = jnp.concatenate(
        [jnp.concatenate([chosen[32 * k + 8 * j : 32 * k + 8 * j + 8] for j in range(4)], axis=1) for k in range(2)], axis=0
    ).astype(BF16)
    chosen = dot(chosen, order_in[...]).astype(BF16)
    for tiles in ((3, 4), (5, 6), (7, 8)):
        got = project(chosen, tiles)
        for k in range(2):
            picked[k, :, 128 * (tiles[0] - 3) : 128 * (tiles[0] - 1)] = got[8 * k : 8 * k + 8].astype(BF16)
    far_ok = (iota((8, 256), 0) >> 2) == ((iota((8, 256), 1) & 127) >> 6)
    for j in range(3):
        for core in range(2):
            at = 3 * core + j
            alive_row = jnp.where(iota((1, 128), 1) < counts[0, 2 * z + core], 1.0, 0.0)
            far = jnp.where(far_ok, dot_t(picked[core, :, 128 * j : 128 * (j + 1)], split_q[at]), -1e30)
            top = jnp.maximum(near_top[at], jnp.max(far, axis=0, keepdims=True))
            keep, far = jnp.exp(near_top[at] - top), jnp.exp(far - top)
            scale = 1.0 / (near_sum[at] * keep + jnp.sum(far, axis=0, keepdims=True))
            mixed = turned_dot(picked[core, :, 384 + 128 * j : 384 + 128 * (j + 1)], far.astype(BF16))
            for k in range(2):
                rows, cols = slice(64 * k, 64 * (k + 1)), slice(128 * k, 128 * (k + 1))
                both = near_mix[at, rows] * keep[:, cols] + mixed[rows, cols]
                att[core, 128 * j + 64 * k : 128 * j + 64 * (k + 1)] = (both * (scale[:, cols] * alive_row)).astype(BF16)
        if j == 0:
            continue
        g = j - 1
        rows = slice(192 * g, 192 * (g + 1))
        both = jnp.concatenate([att[0, rows], att[1, rows]], axis=1)
        for t in range(0, 4, 2):
            got = dot(both, cot[:, :, 128 * t : 128 * (t + 2)].reshape(256, 256))
            for k in range(2):
                terms[t + k, 4 * g : 4 * g + 4] = got[:, 128 * k : 128 * (k + 1)].astype(BF16).reshape(4, 2, 3, 8, 128)
        for d in (2, 1, 3):
            t, where = a_peer(d)
            send(terms.at[t, 4 * g : 4 * g + 4], across.at[d - 1, 4 * g : 4 * g + 4], 39 + g, 55 + g, where)
    att_all[c] = att[c]
    send(att.at[other], att_all.at[c], 37, 5, {"c": other})
    along_b(7)

    for g in range(2):
        rows = slice(4 * g, 4 * (g + 1))
        with jax.named_scope(f"w_across{g}"):
            drain(across.at[:, rows], recv_sem.at[55 + g])
        total = terms[a, rows].astype(F32)
        for d in range(3):
            total = total + across[d, rows].astype(F32)
        summed[rows] = total.astype(BF16)

        def reduce_z(k, _):
            for core in range(2):

                @pl.when((8 * c + k) * 2 + core != me)
                def _():
                    send(summed.at[k, core], along.at[z], 41, 57, {"z": 8 * c + k, "c": core})

            return 0

        lax.fori_loop(4 * g, 4 * (g + 1), reduce_z, 0)
    mine = z // 8 == c

    @pl.when(mine)
    def _():
        along[z] = summed[z - 8 * c, c]

    relay(7)
    with jax.named_scope("w_along"):

        @pl.when(mine)
        def _():
            drain(along.at[0:15], recv_sem.at[57])

        @pl.when(jnp.logical_not(mine))
        def _():
            drain(along, recv_sem.at[57])

    total = along[0].astype(F32)
    for k in range(1, NZ):
        total = total + along[k].astype(F32)
    sender = z // 8
    summed_piece = (1 - sender) * core_pieces[0][0] + sender * core_pieces[1][0]
    final[summed_piece] = total.astype(BF16)

    def show(k, _):
        send(final.at[summed_piece], final.at[summed_piece], 42, 58, plane_peer(k))
        return 0

    lax.fori_loop(1, 16, show, 0)
    last(7)
    crossed(7)
    drain(att_all.at[0], recv_sem.at[5])
    attended = turned_dot(att_all[...].reshape(768, 128), order_out[...]).astype(BF16)
    for t in range(0, 4, 2):
        total = hidden[:, 128 * t : 128 * (t + 2)]
        for i in range(3):
            w = jnp.concatenate([unit(4 * i + t, 2), unit(4 * i + t + 1, 2)], axis=1)
            total = total + dot(attended[:, 256 * i : 256 * (i + 1)], w)
        layer[0, :, 128 * t : 128 * (t + 2)] = total.astype(BF16)

    drain(asked.at[0:31], send_sem.at[0])
    drain(cot.at[0], send_sem.at[1])
    drain(table.at[0:31], send_sem.at[2])
    drain(shorts.at[0:31], send_sem.at[3])
    for n, (lo, hi, s0, s1, far) in CHUNKS.items():
        drain(held.at[0, lo:hi, 0, max(s0, 1) : s1], send_sem.at[5 + n])
        drain(held.at[0:3, lo:hi, 0, s0:s1], send_sem.at[13 + n])
        if not far:
            drain(held.at[0 : 12 if n in RELAYED else 8, lo:hi, 0, s0:s1], send_sem.at[21 + n])
        drain(held.at[0 : crossings(n), lo:hi, 0, s0:s1], send_sem.at[29 + n])
    for n, (s0, s1, far) in SPLIT.items():
        drain(arrivals(n), send_sem.at[5 + n])
        drain(part_in(n, 0, 3), send_sem.at[13 + n])
        if not far:
            drain(part_in(n, 0, 8), send_sem.at[21 + n])
    drain(chosen_hot.at[0], send_sem.at[4])
    drain(normed_all.at[0], send_sem.at[38])
    drain(att_all.at[0], send_sem.at[37])
    for g in range(2):
        drain(across.at[:, 4 * g : 4 * (g + 1)], send_sem.at[39 + g])

    with jax.named_scope("w_final"):
        drain(final.at[0:15], recv_sem.at[58])
    factor = (16 * 4096) ** -0.5
    for t in range(4):
        total = final[t].astype(F32)
        for k in range(1, 4):
            total = total + final[4 * k + t].astype(F32)
        grad[:, 128 * t : 128 * (t + 1)] = total.reshape(24, 128) * factor


    @pl.when(mine)
    def _():
        drain(along.at[0:15], send_sem.at[41])

    @pl.when(jnp.logical_not(mine))
    def _():
        drain(along, send_sem.at[41])

    drain(final.at[0:15], send_sem.at[42])


def shards(feats, near_map, wanted, counts, choice, conv, gain, inw, outw, cot):
    vmem = pl.BlockSpec(memory_space=pltpu.VMEM)
    hbm = pl.BlockSpec(memory_space=pltpu.HBM)
    v = pltpu.VMEM
    return pl.pallas_call(
        kernel,
        name="layer",
        out_shape=(jax.ShapeDtypeStruct((1, 128, 512), BF16), jax.ShapeDtypeStruct((24, 512), F32)),
        in_specs=[hbm] * 10,
        out_specs=(vmem, vmem),
        scratch_shapes=[
            v((128, 256), BF16),
            v((6, 1, 128), jnp.int32),
            v((1, 1, 8, 32), jnp.int32),
            pltpu.SMEM((1, 32), jnp.int32),
            pltpu.SMEM((1, 2, 4), jnp.int32),
            v((1, 512), F32),
            v((2, 128, 128), F32),
            v((32, 1, 128), jnp.int32),
            v((32, 1, 128), jnp.int32),
            v((48, 8, 256), BF16),
            v((32, 8, 256), BF16),
            v((128, 256), BF16),
            v((768, 384), BF16),
            v((6, 128, 256), BF16),
            v((3, 8, 128), BF16),
            v((2, 8, 128), BF16),
            v((2, 2, 8, 128), BF16),
            v((16, 3, 2, NZ, 8, 128), BF16),
            v((16, 2, NZ, 8, 128), BF16),
            v((128, 512), F32),
            v((2, 128, 512), BF16),
            v((256, 1152), BF16),
            v((8, 128), F32),
            v((32, 8, 128), BF16),
            v((2, 32, 256), BF16),
            v((2, 8, 768), BF16),
            v((6, 256, 128), BF16),
            v((6, 128, 128), F32),
            v((6, 1, 256), F32),
            v((6, 1, 256), F32),
            v((2, 128, 512), BF16),
            v((2, 384, 128), BF16),
            v((2, 384, 128), BF16),
            v((4, 8, 2, 3, 8, 128), BF16),
            v((3, 8, 2, 3, 8, 128), BF16),
            v((8, 2, 3, 8, 128), BF16),
            v((NZ, 3, 8, 128), BF16),
            v((16, 3, 8, 128), BF16),
            v((256, 256), BF16),
            v((512, 512), BF16),
            v((768, 768), BF16),
            pltpu.SemaphoreType.DMA((20,)),
            pltpu.SemaphoreType.DMA((43,)),
            pltpu.SemaphoreType.DMA((59,)),
        ],
        compiler_params=pltpu.CompilerParams(
            collective_id=0, has_side_effects=True, vmem_limit_bytes=VMEM
        ),
    )(
        *(
            pltpu.with_memory_space_constraint(array, pltpu.HBM)
            for array in (
                feats, near_map.transpose(2, 0, 1), wanted.swapaxes(2, 3), counts, choice, conv, gain.reshape(1, -1), inw, outw, cot
            )
        )
    )


def solution(mesh):
    space = ("z", "c")
    dp = ("y", "x")
    torus = Mesh(mesh.devices.reshape(4, 4, 16, 2), dp + space)
    return jax.shard_map(
        shards,
        mesh=torus,
        in_specs=(
            P(dp, space, None),
            P(dp, space, None),
            P(dp, space, None, None),
            P(dp, None),
            P(dp, space, None),
            P(None, space, None),
            P(),
            P(space, None),
            P(space, None),
            P(dp, space, None),
        ),
        out_specs=(P(dp, space, None), P(space, None)),
        check_vma=False,
    )
```

time: 71.6 us -> 70.1 us (0.979)
  Pallas kernels: 69.1 us -> 68.1 us
    pallas_call x1, Pallas kernels: 69.1 us -> 68.1 us  [shards(): pl.pallas_call(kernel, name='layer', out_shape=(jax.ShapeDtypeStruct((1,...]
where the time goes in v4:
time: 70.1 us; the launch traced here: 70 us
  Pallas kernels  68.1 us (97%)
  local copies, waits for them, and re-layouts  1.28 us (2%)
    pallas_call x1, Pallas kernels, shards(): pl.pallas_call(kernel, name='layer', out_shape=(jax.ShapeDtypeStruct((1,...  68.1 us

profile of v4, /device:TPU:1, one launch (start us, length us, event | category | flops | bytes accessed | tf_op | source)
XLA Modules:
  0.0 70.0 jit_solution(6479148214692215399)
XLA Ops:
  0.6 68.1 %layer.1 = (bf16[1,128,512]{2,1,0:T(8,128)(2,1)S(1)}, f32[24,512]{1,0:T(8,128)S(1)}) custom-call(bf16[1,128,256]{2,1,0:T(8,128)(2,1)} %feats_h.1, s32[6,1,128]{2,1,0:T(1,128)} %bitcast.4, s32[1,1,8,32]{3,2,1,0:T(8,128)} %bitcast.3, s32[1,32]{1,0:T(1,128)} %counts_h.1, s32[1,2,4]{2,1,0:T(2,128)} %choice_h.1, bf16[7,8,512]{2,1,0:T(8,128)(2,1)} %conv_h.1, ...), custom_call_target="tpu_custom_call" | custom-call | tf_op jit(solution)/shard_map/layer/pallas_call | solution.py:576
  68.7 0.7 copy.14
  69.4 0.6 copy.15

commit v5 on v4

--- a/solution.py
+++ b/solution.py
@@ -13,7 +13,8 @@
 VMEM = 48 * 1024 * 1024
 CHUNKS = {0: (0, 2, 0, 8, 0), 1: (0, 2, 8, 16, 0), 2: (0, 2, 0, 8, 1), 3: (0, 2, 8, 16, 1), 7: (2, 3, 0, 16, 0)}
 RELAYED = (7,)
-SPLIT = {4: (0, 8, 0), 5: (8, 16, 0), 6: (0, 16, 1)}
+SPLIT = {4: (0, 8, 0), 5: (8, 16, 0), 6: (0, 8, 1), 8: (8, 16, 1)}
+LAST = 8
 
 
 def iota(shape, dim):
@@ -198,21 +199,27 @@
 
         lax.fori_loop(max(s0, 1), s1, one, 0)
 
+    def along_z(n):
+        return (43, 59) if n == LAST else (5 + n, 7 + n)
+
+    def along_axis(n):
+        return (44, 60) if n == LAST else (13 + n, 15 + n)
+
     def spread_in(n):
         s0, s1, far = SPLIT[n]
 
         def one(slot, _):
             for h in range(2):
-                send(staged_in.at[h, far], split_in.at[core_pieces[h][far], c, slot], 5 + n, 7 + n, {"z": z_of(slot), "c": h})
+                send(staged_in.at[h, far], split_in.at[core_pieces[h][far], c, slot], *along_z(n), {"z": z_of(slot), "c": h})
             return 0
 
         if s0 == 0:
             p = (1 - other) * core_pieces[0][far] + other * core_pieces[1][far]
-            send(staged_in.at[other, far], split_in.at[p, c, 0], 5 + n, 7 + n, {"c": other})
+            send(staged_in.at[other, far], split_in.at[p, c, 0], *along_z(n), {"c": other})
         lax.fori_loop(max(s0, 1), s1, one, 0)
 
     def arrivals(n):
-        return (split_in.at[0, 0, 0:15], split_in.at[0, 0], shorts.at[0:31])[n - 4]
+        return split_in.at[0, 0, 0 : 15 if SPLIT[n][0] == 0 else 16]
 
     far_first(ask)
     send(asks.at[z * 2 + other], asked.at[me], 0, 0, {"c": other})
@@ -279,14 +286,14 @@
 
     def split_a(n):
         with jax.named_scope(f"w_z{n}"):
-            drain(arrivals(n), recv_sem.at[7 + n])
+            drain(arrivals(n), recv_sem.at[along_z(n)[1]])
         some = part_in(n, piece_far if SPLIT[n][2] else piece, 1)
         for d in (2, 1, 3):
-            send(some, some, 13 + n, 15 + n, a_peer(d)[1])
+            send(some, some, *along_axis(n), a_peer(d)[1])
 
     def split_b(n):
         with jax.named_scope(f"w_a{n}"):
-            drain(part_in(n, 0, 3), recv_sem.at[15 + n])
+            drain(part_in(n, 0, 3), recv_sem.at[along_axis(n)[1]])
         if not SPLIT[n][2]:
             for k, d in enumerate((1, 3)):
                 send(part_in(n, b * 4, 4), part_in(n, b * 4, 4), 21 + n, 23 + 8 * k + n, b_peer(d)[1])
@@ -322,6 +329,7 @@
 
     far_first(answer)
     send(answers.at[z * 2 + other], table.at[16 + me], 2, 2, {"c": other})
+    spread_in(8)
     spread_in(6)
     spread(7)
 
@@ -383,12 +391,13 @@
     normed_all[c] = dot(normed, order_in[...]).astype(BF16)
     send(normed_all.at[c], normed_all.at[c], 38, 6, {"c": other})
     split_a(6)
+    split_a(8)
     split_end(4)
-    along_a(7)
     with jax.named_scope("w_norm"):
         drain(normed_all.at[0], recv_sem.at[6])
     split_end(5)
     split_b(6)
+    split_b(8)
 
     def unit_in(tile, i):
         if tile < 8:
@@ -424,6 +433,7 @@
             mixed = turned_dot(qkv[rows, 768 + 128 * j : 768 + 128 * (j + 1)], near.astype(BF16))
             near_mix[at, 0:64] = mixed[0:64, 0:128]
             near_mix[at, 64:128] = mixed[64:128, 128:256]
+    along_a(7)
     drain(chosen_hot.at[0], recv_sem.at[4])
     drain(cot.at[0], recv_sem.at[1])
 
@@ -466,7 +476,6 @@
             send(terms.at[t, 4 * g : 4 * g + 4], across.at[d - 1, 4 * g : 4 * g + 4], 39 + g, 55 + g, where)
     att_all[c] = att[c]
     send(att.at[other], att_all.at[c], 37, 5, {"c": other})
-    along_b(7)
 
     for g in range(2):
         rows = slice(4 * g, 4 * (g + 1))
@@ -487,6 +496,7 @@
             return 0
 
         lax.fori_loop(4 * g, 4 * (g + 1), reduce_z, 0)
+    along_b(7)
     mine = z // 8 == c
 
     @pl.when(mine)
@@ -511,11 +521,10 @@
     summed_piece = (1 - sender) * core_pieces[0][0] + sender * core_pieces[1][0]
     final[summed_piece] = total.astype(BF16)
 
-    def show(k, _):
-        send(final.at[summed_piece], final.at[summed_piece], 42, 58, plane_peer(k))
-        return 0
-
-    lax.fori_loop(1, 16, show, 0)
+    for dy, dx in sorted(((dy, dx) for dy in range(4) for dx in range(4)), key=lambda d: -(d[0] * (4 - d[0]) + d[1] * (4 - d[1]))):
+        if (dy, dx) != (0, 0):
+            where = {"y": lax.rem(y + dy, 4), "x": lax.rem(x + dx, 4)}
+            send(final.at[summed_piece], final.at[summed_piece], 42, 58, where)
     last(7)
     crossed(7)
     drain(att_all.at[0], recv_sem.at[5])
@@ -538,8 +547,8 @@
             drain(held.at[0 : 12 if n in RELAYED else 8, lo:hi, 0, s0:s1], send_sem.at[21 + n])
         drain(held.at[0 : crossings(n), lo:hi, 0, s0:s1], send_sem.at[29 + n])
     for n, (s0, s1, far) in SPLIT.items():
-        drain(arrivals(n), send_sem.at[5 + n])
-        drain(part_in(n, 0, 3), send_sem.at[13 + n])
+        drain(arrivals(n), send_sem.at[along_z(n)[0]])
+        drain(part_in(n, 0, 3), send_sem.at[along_axis(n)[0]])
         if not far:
             drain(part_in(n, 0, 8), send_sem.at[21 + n])
     drain(chosen_hot.at[0], send_sem.at[4])
@@ -547,6 +556,14 @@
     drain(att_all.at[0], send_sem.at[37])
     for g in range(2):
         drain(across.at[:, 4 * g : 4 * (g + 1)], send_sem.at[39 + g])
+
+    @pl.when(mine)
+    def _():
+        drain(along.at[0:15], send_sem.at[41])
+
+    @pl.when(jnp.logical_not(mine))
+    def _():
+        drain(along, send_sem.at[41])
 
     with jax.named_scope("w_final"):
         drain(final.at[0:15], recv_sem.at[58])
@@ -556,15 +573,6 @@
         for k in range(1, 4):
             total = total + final[4 * k + t].astype(F32)
         grad[:, 128 * t : 128 * (t + 1)] = total.reshape(24, 128) * factor
-
-
-    @pl.when(mine)
-    def _():
-        drain(along.at[0:15], send_sem.at[41])
-
-    @pl.when(jnp.logical_not(mine))
-    def _():
-        drain(along, send_sem.at[41])
 
     drain(final.at[0:15], send_sem.at[42])
 
@@ -622,8 +630,8 @@
             v((512, 512), BF16),
             v((768, 768), BF16),
             pltpu.SemaphoreType.DMA((20,)),
-            pltpu.SemaphoreType.DMA((43,)),
-            pltpu.SemaphoreType.DMA((59,)),
+            pltpu.SemaphoreType.DMA((45,)),
+            pltpu.SemaphoreType.DMA((61,)),
         ],
         compiler_params=pltpu.CompilerParams(
             collective_id=0, has_side_effects=True, vmem_limit_bytes=VMEM

time: 70.1 us -> 68.1 us (0.971)
  Pallas kernels: 68.1 us -> 66.1 us
    pallas_call x1, Pallas kernels: 68.1 us -> 66.1 us  [shards(): pl.pallas_call(kernel, name='layer', out_shape=(jax.ShapeDtypeStruct((1,...]
where the time goes in v5:
time: 68.1 us; the launch traced here: 68 us
  Pallas kernels  66.1 us (97%)
  local copies, waits for them, and re-layouts  1.28 us (2%)
    pallas_call x1, Pallas kernels, shards(): pl.pallas_call(kernel, name='layer', out_shape=(jax.ShapeDtypeStruct((1,...  66.1 us

profile of v5, /device:TPU:1, one launch (start us, length us, event | category | flops | bytes accessed | tf_op | source)
XLA Modules:
  0.0 68.0 jit_solution(7930900601844613908)
XLA Ops:
  0.6 66.1 %layer.1 = (bf16[1,128,512]{2,1,0:T(8,128)(2,1)S(1)}, f32[24,512]{1,0:T(8,128)S(1)}) custom-call(bf16[1,128,256]{2,1,0:T(8,128)(2,1)} %feats_h.1, s32[6,1,128]{2,1,0:T(1,128)} %bitcast.4, s32[1,1,8,32]{3,2,1,0:T(8,128)} %bitcast.3, s32[1,32]{1,0:T(1,128)} %counts_h.1, s32[1,2,4]{2,1,0:T(2,128)} %choice_h.1, bf16[7,8,512]{2,1,0:T(8,128)(2,1)} %conv_h.1, ...), custom_call_target="tpu_custom_call" | custom-call | tf_op jit(solution)/shard_map/layer/pallas_call | solution.py:584
  66.7 0.7 copy.14
  67.4 0.6 copy.15

commit v6 on v5

--- a/solution.py
+++ b/solution.py
@@ -331,7 +331,6 @@
     send(answers.at[z * 2 + other], table.at[16 + me], 2, 2, {"c": other})
     spread_in(8)
     spread_in(6)
-    spread(7)
 
     along_a(1)
     along_b(0)
@@ -387,6 +386,7 @@
 
     far_first(tell)
     send(shorts.at[me], shorts.at[me], 3, 3, {"c": other})
+    spread(7)
 
     normed_all[c] = dot(normed, order_in[...]).astype(BF16)
     send(normed_all.at[c], normed_all.at[c], 38, 6, {"c": other})
@@ -433,7 +433,6 @@
             mixed = turned_dot(qkv[rows, 768 + 128 * j : 768 + 128 * (j + 1)], near.astype(BF16))
             near_mix[at, 0:64] = mixed[0:64, 0:128]
             near_mix[at, 64:128] = mixed[64:128, 128:256]
-    along_a(7)
     drain(chosen_hot.at[0], recv_sem.at[4])
     drain(cot.at[0], recv_sem.at[1])
 
@@ -476,6 +475,7 @@
             send(terms.at[t, 4 * g : 4 * g + 4], across.at[d - 1, 4 * g : 4 * g + 4], 39 + g, 55 + g, where)
     att_all[c] = att[c]
     send(att.at[other], att_all.at[c], 37, 5, {"c": other})
+    along_a(7)
 
     for g in range(2):
         rows = slice(4 * g, 4 * (g + 1))

time: 68.1 us -> 67.2 us (0.987)
  Pallas kernels: 66.1 us -> 65.1 us
    pallas_call x1, Pallas kernels: 66.1 us -> 65.1 us  [shards(): pl.pallas_call(kernel, name='layer', out_shape=(jax.ShapeDtypeStruct((1,...]
where the time goes in v6:
time: 67.2 us; the launch traced here: 67.1 us
  Pallas kernels  65.1 us (97%)
  local copies, waits for them, and re-layouts  1.28 us (2%)
    pallas_call x1, Pallas kernels, shards(): pl.pallas_call(kernel, name='layer', out_shape=(jax.ShapeDtypeStruct((1,...  65.1 us

profile of v6, /device:TPU:1, one launch (start us, length us, event | category | flops | bytes accessed | tf_op | source)
XLA Modules:
  0.0 67.1 jit_solution(7232161705238701805)
XLA Ops:
  0.6 65.1 %layer.1 = (bf16[1,128,512]{2,1,0:T(8,128)(2,1)S(1)}, f32[24,512]{1,0:T(8,128)S(1)}) custom-call(bf16[1,128,256]{2,1,0:T(8,128)(2,1)} %feats_h.1, s32[6,1,128]{2,1,0:T(1,128)} %bitcast.4, s32[1,1,8,32]{3,2,1,0:T(8,128)} %bitcast.3, s32[1,32]{1,0:T(1,128)} %counts_h.1, s32[1,2,4]{2,1,0:T(2,128)} %choice_h.1, bf16[7,8,512]{2,1,0:T(8,128)(2,1)} %conv_h.1, ...), custom_call_target="tpu_custom_call" | custom-call | tf_op jit(solution)/shard_map/layer/pallas_call | solution.py:584
  65.8 0.7 copy.14
  66.4 0.6 copy.15
